TPU v7x, 256 devices: a whole 4x4x8 slice. The times are simulated.
256 devices in a mesh: ep: 64 (over z, y, core), fsdp: 4 (over x).
Axes of the slice: x: 4, y: 4, z: 8, core: 2. Of those that a mesh axis runs over, the one named last changes fastest.
Arguments:
- w_down: float32 [64, 1408, 2048], P('ep', None, 'fsdp'), may hold values from -0.21875 to 0.21875
- avg_down: float32 [64, 1408, 2048], P('ep', None, 'fsdp'), may hold values from -0.15625 to 0.15625
- router_weight: float32 [2048, 64], P('fsdp', 'ep'), may hold values from -0.125 to 0.125
- router_gain: float32 [2048], P('fsdp'), may hold values from 0.25 to 1.75
Outputs:
- serve_down: bfloat16 [64, 1408, 2048], P('ep')
- scale_down: float32 [64, 1408], P('ep')
- serve_router: bfloat16 [2048, 64], replicated
- fresh_down: float32 [64, 1408, 2048], P('ep', None, 'fsdp')
All inputs are finite; a program needn't handle non-finite values. Where the computation divides by a largest or mean magnitude, that divisor is 1e-20 or more.
Results may differ from a plain program's by a relative error of at most 0.001.
Values may be sent and summed in bfloat16 or wider, within the bound.
A program may use at most 64 MiB of HBM per device.

v0:
```python
import jax
import jax.numpy as jnp
from jax import lax
from jax.sharding import PartitionSpec as P


def sent_to_all(value, axis):
    copies = jnp.broadcast_to(value, (lax.axis_size(axis), *value.shape))
    return lax.all_to_all(copies, axis, split_axis=0, concat_axis=0, tiled=True)


def of_everyone(value, axis):
    everything = sent_to_all(value, axis)
    return jnp.max(everything, axis=0)


def in_order(blocks, dim):
    blocks = jnp.moveaxis(blocks, 0, dim)
    dims = blocks.shape
    return blocks.reshape(*dims[:dim], dims[dim] * dims[dim + 1], *dims[dim + 2 :])


def collect(value, axis, dim):
    return in_order(sent_to_all(value, axis), dim)


def body(w_down, avg_down, router_weight, router_gain):
    fresh_down = 0.5 * avg_down + 0.5 * w_down
    scale_down = of_everyone(jnp.max(jnp.abs(fresh_down), axis=2), "fsdp")
    narrow_down = (fresh_down / jnp.expand_dims(scale_down, 2)).astype(jnp.bfloat16)
    serve_down = lax.all_gather(narrow_down, "fsdp", axis=2, tiled=True)
    part_router = (router_weight * router_gain[:, None]).astype(jnp.bfloat16)
    row_router = lax.all_gather(part_router, "fsdp", axis=0, tiled=True)
    serve_router = collect(row_router, "ep", 1)
    return (serve_down, scale_down, serve_router, fresh_down)


def solution(mesh):
    placed = (P("ep", None, "fsdp"), P("ep", None, "fsdp"), P("fsdp", "ep"), P("fsdp"))
    return jax.shard_map(
        body,
        mesh=mesh,
        in_specs=placed,
        out_specs=(P("ep", None, None), P("ep", None), P(), P("ep", None, "fsdp")),
        check_vma=False,
    )
```

profile of v0, /device:TPU:8, one launch (start us, length us, event | category | flops | bytes accessed | tf_op | source)
XLA Modules:
  0.0 99.3 jit_solution(13331226451269503026)
XLA Ops:
  7.2 0.0 all-gather.2.cloned.1.call-start
  7.2 3.2 %abs_reduce_fusion = (f32[1408]{0:T(1024)S(1)}, f32[1,1408,512]{2,1,0:T(8,128)S(1)}) fusion(f32[1,1408,512]{2,1,0:T(8,128)} %param.5, f32[1,1408,512]{2,1,0:T(8,128)} %param.4), kind=kLoop, calls=%fused_computation.1 | loop fusion | flops 2882176 | bytes 8656384 | tf_op jit(solution)/shard_map/reduce_max | solution.py:29
  10.4 0.0 copy-start
  10.4 9.5 %all_to_all.10 = f32[4,1,1408]{2,1,0:T(1,128)S(1)} all-to-all(f32[4,1,1408]{2,1,0:T(1,128)S(1)} %broadcast_in_dim.10), channel_id=1, replica_groups=mesh['ep'=64,'fsdp'=4] {'fsdp'}, dimensions={0} | all-to-all | bytes 45056 | tf_op jit(solution)/shard_map/all_to_all | solution.py:9
  19.9 0.0 copy-start.1
  19.9 0.0 copy-start.2
  19.9 1.4 %divide_convert_fusion = bf16[1,1408,512]{2,1,0:T(8,128)(2,1)} fusion(f32[1,1408,512]{2,1,0:T(8,128)S(1)} %get-tuple-element.13, f32[1408]{0:T(1024)S(1)} %reduce_max.21), kind=kLoop, calls=%fused_computation | loop fusion | flops 1441792 | bytes 4331008 | tf_op jit(solution)/shard_map/convert_element_type | solution.py:30
  21.3 0.0 all-gather.2.cloned.1.call-update
  21.3 0.0 copy-done
  21.3 0.0 copy-done.1
  21.4 0.0 copy-done.2
  21.4 10.4 %all_gather.9 = bf16[2048,1]{0,1:T(2,128)(2,1)S(1)} all-gather(bf16[512,1]{0,1:T(2,128)(2,1)S(1)} %multiply_convert_fusion), channel_id=1, replica_groups=mesh['ep'=64,'fsdp'=4] {'fsdp'}, dimensions={0}, use_global_device_ids=true | all-gather | bytes 5120 | tf_op jit(solution)/shard_map/all_gather | solution.py:33
  31.9 0.3 broadcast_bitcast_fusion
  32.1 0.5 broadcast.12
  32.6 2.2 %reduce.3 = bf16[64,2048]{1,0:T(8,128)(2,1)S(1)} reduce(bf16[64,1,2048]{2,1,0:T(2,128)(2,1)S(1)} %broadcast_bitcast_fusion, bf16[]{:T(256)} %broadcast.12), dimensions={1}, to_apply=%broadcast_bitcast_fusion.reduce_sub_computation | reduce | bytes 524290
  34.8 0.9 reshape.22
  35.7 12.1 %all-to-all-start.1 = ((bf16[64,2,1024]{2,1,0:T(2,128)(2,1)}), bf16[64,2,1024]{2,1,0:T(2,128)(2,1)S(1)}, u32[]{:S(2)}, u32[]{:S(2)}) async-start(bf16[64,2,1024]{2,1,0:T(2,128)(2,1)} %reshape.22), calls=%async_computation.1 | async-start | bytes 524288 | tf_op jit(solution)/shard_map/all_to_all | solution.py:9
  47.8 0.6 reduce_max.22
  48.4 11.6 %all-to-all-done.1 = bf16[64,2,1024]{2,1,0:T(2,128)(2,1)S(1)} async-done(((bf16[64,2,1024]{2,1,0:T(2,128)(2,1)}), bf16[64,2,1024]{2,1,0:T(2,128)(2,1)S(1)}, u32[]{:S(2)}, u32[]{:S(2)}) %all-to-all-start.1) | async-done | bytes 262176 | tf_op jit(solution)/shard_map/all_to_all | solution.py:9
  60.0 0.2 reshape.23
  60.2 0.9 copy.14
  61.1 25.2 %all-gather.2.cloned.1.call-done = bf16[1,1408,2048]{2,1,0:T(8,128)(2,1)} async-done(((bf16[1,1408,512]{2,1,0:T(8,128)(2,1)}), bf16[1,1408,2048]{2,1,0:T(8,128)(2,1)}) %all-gather.2.cloned.1.call-update) | async-done | bytes 5767184 | tf_op jit(solution)/shard_map/all_gather | solution.py:31
  86.3 6.2 %copy.16 = bf16[1,1408,2048]{2,1,0:T(8,128)(2,1)} copy(bf16[1,1408,2048]{2,1,0:T(8,128)(2,1)} %all-gather.2.cloned.1.call-done) | data formatting | bytes 11534336
  (4 shorter events, 0.1 us)
Async XLA Ops:
  7.2 79.1 %all-gather.2.cloned.1.call-start = ((), (), s32[]{:S(2)}) async-start(), calls=%async_computation.2 | async-start | bytes 7208960 | tf_op jit(solution)/shard_map/all_gather | solution.py:31
  10.4 11.0 %copy-start = (f32[1,1408,512]{2,1,0:T(8,128)}, f32[1,1408,512]{2,1,0:T(8,128)S(1)}, u32[]{:S(2)}) copy-start(f32[1,1408,512]{2,1,0:T(8,128)S(1)} %get-tuple-element.13) | copy-start | bytes 8650756
  19.9 1.4 %copy-start.1 = (f32[512,1]{0,1:T(1,128)S(1)}, f32[512,1]{0,1:T(1,128)}, u32[]{:S(2)}) copy-start(f32[512,1]{0,1:T(1,128)} %param.6) | copy-start | bytes 6148
  19.9 1.4 %copy-start.2 = (f32[512]{0:T(512)S(1)}, f32[512]{0:T(512)}, u32[]{:S(2)}) copy-start(f32[512]{0:T(512)} %param.7) | copy-start | bytes 6148
  35.7 24.3 %all-to-all-start.1 = ((bf16[64,2,1024]{2,1,0:T(2,128)(2,1)}), bf16[64,2,1024]{2,1,0:T(2,128)(2,1)S(1)}, u32[]{:S(2)}, u32[]{:S(2)}) async-start(bf16[64,2,1024]{2,1,0:T(2,128)(2,1)} %reshape.22), calls=%async_computation.1 | async-start | bytes 524288 | tf_op jit(solution)/shard_map/all_to_all | solution.py:9
Sparse Core Ops, SparseCore 0:
  21.5 64.8 all-gather.1
where the time goes:
time: 100 us; the launch traced here: 99.3 us
  waiting for transfers between devices  36.8 us (37%)
  blocking collectives  19.9 us (20%)
  between operations  14.1 us (14%)
  starting transfers between devices  12.1 us (12%)
  local copies, waits for them, and re-layouts  9.53 us (10%)
  other arithmetic  6.74 us (7%)
    all_gather x1, waiting for transfers between devices, body(): serve_down = lax.all_gather(narrow_down, 'fsdp', axis=2, tiled=True)  25.2 us
    all_to_all x1, starting transfers between devices, sent_to_all(): return lax.all_to_all(copies, axis, split_axis=0, concat_axis=0, tiled=True)  12.1 us
    all_to_all x1, waiting for transfers between devices, sent_to_all(): return lax.all_to_all(copies, axis, split_axis=0, concat_axis=0, tiled=True)  11.6 us
    all_gather x1, blocking collectives, body(): row_router = lax.all_gather(part_router, 'fsdp', axis=0, tiled=True)  10.4 us
    all_to_all x1, blocking collectives, sent_to_all(): return lax.all_to_all(copies, axis, split_axis=0, concat_axis=0, tiled=True)  9.49 us
    unnamed x11, local copies, waits for them, and re-layouts  8.06 us
    reduce_max x1, other arithmetic, body(): scale_down = of_everyone(jnp.max(jnp.abs(fresh_down), axis=2), 'fsdp')  3.15 us
    unnamed x1, other arithmetic  2.15 us
  transfers between devices with their start and end apart: 2, of which 2 were waited for; matrix products, arithmetic and copies ran while one was open for 6% of the time, Pallas kernels for 0%

commit v1 on v0

v1 whole, which is shorter than its diff:
```python
import jax
import jax.numpy as jnp
from jax import lax
from jax.experimental import pallas as pl
from jax.experimental.pallas import tpu as pltpu
from jax.sharding import PartitionSpec as P

MESH = pl.DeviceIdType.MESH
F32, BF16 = jnp.float32, jnp.bfloat16
NX, NY, NZ, NC = 4, 4, 8, 2
ROWS, COLS = 1408, 512
WIDE = NX * COLS
HALF = COLS // 2
BLK = 128
NB = ROWS // BLK


def rows_of(b):
    return pl.ds(pl.multiple_of(b * BLK, BLK), BLK)


def gather_kernel(
    w_hbm, a_hbm, rw_hbm, gain_hbm, serve, fresh, scale, router,
    wbuf, abuf, rw, gain, m0, m1, piece, wide,
    load_sem, small_sem, m_send, m_recv, own_send, own_recv, fwd_send, fwd_recv,
    r0_send, r0_recv, r1_send, r1_recv, r2_send, r2_recv, r3_send, r3_recv,
):
    x, e = lax.axis_index("fsdp"), lax.axis_index("ep")
    right, far, left = lax.rem(x + 1, NX), lax.rem(x + 2, NX), lax.rem(x + 3, NX)
    lo = lax.rem(e, NY * NC)
    z, y, c = e // (NY * NC), lo // NC, lax.rem(lo, NC)
    x_peers = ({"fsdp": right}, {"fsdp": left}, {"fsdp": far})
    mate = {"ep": e + 1 - 2 * c}
    y_up = {"ep": z * (NY * NC) + lax.rem(y + 1, NY) * NC + c}
    y_down = {"ep": z * (NY * NC) + lax.rem(y + NY - 1, NY) * NC + c}
    z_up = {"ep": lax.rem(z + 1, NZ) * (NY * NC) + lo}
    z_down = {"ep": lax.rem(z + NZ - 1, NZ) * (NY * NC) + lo}

    def load(b, k):
        src, dst = ((w_hbm, wbuf), (a_hbm, abuf))[k]
        return pltpu.make_async_copy(src.at[rows_of(b)], dst.at[rows_of(b)], load_sem.at[k, b])

    def start_load(b, carry):
        load(b, 0).start()
        load(b, 1).start()
        return carry

    def remote(src, dst, send, recv, peer):
        return pltpu.make_async_remote_copy(
            src_ref=src, dst_ref=dst, send_sem=send, recv_sem=recv, device_id=peer, device_id_type=MESH
        )

    small = [
        pltpu.make_async_copy(rw_hbm, rw, small_sem.at[0]),
        pltpu.make_async_copy(gain_hbm, gain, small_sem.at[1]),
    ]
    start_load(0, 0)
    for copy in small:
        copy.start()
    lax.fori_loop(1, NB, start_load, 0)

    barrier = pltpu.get_barrier_semaphore()
    peers = (*x_peers, mate, y_up, y_down, z_up, z_down)
    for peer in peers:
        pl.semaphore_signal(barrier, inc=1, device_id=peer, device_id_type=MESH)

    def average(b):
        load(b, 0).wait()
        load(b, 1).wait()
        here = rows_of(b)
        top = None
        for k in range(COLS // 128):
            lanes = pl.ds(k * 128, 128)
            value = 0.5 * abuf[here, lanes] + 0.5 * wbuf[here, lanes]
            fresh[here, lanes] = value
            top = jnp.abs(value) if top is None else jnp.maximum(top, jnp.abs(value))
        return jnp.max(top.T, axis=0, keepdims=True)

    m0[x] = average(0)
    for copy in small:
        copy.wait()
    part = rw[...] * gain[...]
    for k in range(NX):
        piece[lo, x, k : k + 1, :] = part[:, k * 128 : (k + 1) * 128]
    pl.semaphore_wait(barrier, len(peers))

    first = [remote(m0.at[x], m0.at[x], m_send.at[0, k], m_recv.at[0, k], x_peers[k]) for k in range(3)]
    rest = [remote(m1.at[x], m1.at[x], m_send.at[1, k], m_recv.at[1, k], x_peers[k]) for k in range(3)]
    r0 = [remote(piece.at[lo, x], piece.at[lo, x], r0_send.at[k], r0_recv.at[k], x_peers[k]) for k in range(3)]
    for copy in first:
        copy.start()
    for copy in r0:
        copy.start()

    def maxima(b, carry):
        m1[x, pl.ds(b - 1, 1), :] = average(b)
        return carry

    lax.fori_loop(1, NB, maxima, 0)
    for copy in rest:
        copy.start()

    mine = x * COLS

    def own(b, h, d):
        ref = serve.at[rows_of(b), pl.ds(pl.multiple_of(mine + h * HALF, HALF), HALF)]
        return remote(ref, ref, own_send.at[d, h, b], own_recv.at[d, h, b], x_peers[d])

    def forward(b, d):
        start = (left if d == 0 else right) * COLS + d * HALF
        ref = serve.at[rows_of(b), pl.ds(pl.multiple_of(start, HALF), HALF)]
        return remote(ref, ref, fwd_send.at[d, b], fwd_recv.at[d, b], x_peers[d])

    def narrow(b, top):
        here = rows_of(b)
        scale[:, pl.ds(pl.multiple_of(b * BLK, BLK), BLK)] = top
        tall = jnp.broadcast_to(top, (BLK, BLK)).T
        for k in range(COLS // 128):
            value = fresh[here, pl.ds(k * 128, 128)] / tall
            serve[here, pl.ds(pl.multiple_of(mine + k * 128, 128), 128)] = value.astype(BF16)

    for copy in first:
        copy.wait_recv()
    narrow(0, jnp.maximum(jnp.maximum(m0[0], m0[1]), jnp.maximum(m0[2], m0[3])))
    own(0, 0, 0).start()
    own(0, 1, 1).start()
    own(0, 1, 0).start()
    own(0, 0, 1).start()
    for copy in rest:
        copy.wait_recv()

    def first_halves(b, carry):
        at = pl.ds(b - 1, 1)
        narrow(b, jnp.maximum(jnp.maximum(m1[0, at], m1[1, at]), jnp.maximum(m1[2, at], m1[3, at])))
        own(b, 0, 0).start()
        own(b, 1, 1).start()
        return carry

    def second_halves(b, carry):
        own(b, 1, 0).start()
        own(b, 0, 1).start()
        return carry

    lax.fori_loop(1, NB, first_halves, 0)
    lax.fori_loop(1, NB, second_halves, 0)

    for copy in r0:
        copy.wait_recv()
    r1 = remote(piece.at[lo], piece.at[lo], r1_send, r1_recv, mate)
    r1.start()
    r1.wait_recv()
    chip = piece.at[pl.ds(y * NC, NC)]
    below = piece.at[pl.ds(lax.rem(y + NY - 1, NY) * NC, NC)]
    r2 = [
        remote(chip, chip, r2_send.at[0], r2_recv.at[0], y_up),
        remote(chip, chip, r2_send.at[1], r2_recv.at[1], y_down),
        remote(below, below, r2_send.at[2], r2_recv.at[2], y_up),
    ]
    r2[0].start()
    r2[1].start()
    r2[0].wait_recv()
    r2[2].start()
    r2[1].wait_recv()
    r2[2].wait_recv()
    for i in range(NY * NC):
        for k in range(WIDE // 128):
            wide[i : i + 1, k * 128 : (k + 1) * 128] = piece[i, k // 4, k % 4 : k % 4 + 1, :]
    router[z] = wide[...].astype(BF16)
    r3 = []
    for k in range(NZ // 2):
        for d, peer in ((0, z_up), (1, z_down)):
            if d == 1 and k == NZ // 2 - 1:
                continue
            plane = router.at[lax.rem(z + (NZ - k if d == 0 else k), NZ)]
            r3.append((k, d, remote(plane, plane, r3_send.at[d, k], r3_recv.at[d, k], peer)))
    for k in range(NZ // 2):
        for step, d, copy in r3:
            if step == k:
                copy.start()
        for step, d, copy in r3:
            if step == k:
                copy.wait_recv()

    def pass_on(b, carry):
        own(b, 0, 0).wait_recv()
        forward(b, 0).start()
        own(b, 1, 1).wait_recv()
        forward(b, 1).start()
        return carry

    lax.fori_loop(0, NB, pass_on, 0)

    def finish(b, carry):
        own(b, 1, 0).wait_recv()
        own(b, 0, 1).wait_recv()
        for d in range(2):
            forward(b, d).wait_recv()
            for h in range(2):
                own(b, h, d).wait_send()
            forward(b, d).wait_send()
        return carry

    lax.fori_loop(0, NB, finish, 0)
    for copy in (*first, *rest, *r0, r1, *r2, *[step[2] for step in r3]):
        copy.wait_send()


def gather(w_down, avg_down, rw, gain):
    dma, any_, vmem = pltpu.SemaphoreType.DMA, pl.BlockSpec(memory_space=pl.ANY), pl.BlockSpec(memory_space=pltpu.VMEM)
    return pl.pallas_call(
        gather_kernel,
        out_shape=(
            pltpu.VMEM((ROWS, WIDE), BF16),
            pltpu.VMEM((ROWS, COLS), F32),
            pltpu.VMEM((1, ROWS), F32),
            pltpu.VMEM((NZ, NY * NC, WIDE), BF16),
        ),
        in_specs=[any_] * 4,
        out_specs=(vmem, vmem, vmem, vmem),
        scratch_shapes=[
            pltpu.VMEM((ROWS, COLS), F32),
            pltpu.VMEM((ROWS, COLS), F32),
            pltpu.VMEM((1, COLS), F32),
            pltpu.VMEM((1, COLS), F32),
            pltpu.VMEM((NX, 1, BLK), F32),
            pltpu.VMEM((NX, NB - 1, BLK), F32),
            pltpu.VMEM((NY * NC, NX, NX, 128), F32),
            pltpu.VMEM((NY * NC, WIDE), F32),
            dma((2, NB)),
            dma((2,)),
            dma((2, 3)),
            dma((2, 3)),
            dma((2, 2, NB)),
            dma((2, 2, NB)),
            dma((2, NB)),
            dma((2, NB)),
            dma((3,)),
            dma((3,)),
            dma,
            dma,
            dma((3,)),
            dma((3,)),
            dma((2, NZ // 2)),
            dma((2, NZ // 2)),
        ],
        compiler_params=pltpu.CompilerParams(
            collective_id=0, has_side_effects=True, vmem_limit_bytes=24 << 20
        ),
        name="gather",
    )(*(pltpu.with_memory_space_constraint(v, pltpu.HBM) for v in (w_down, avg_down, rw, gain)))


PIECES = 8


def store_kernel(serve, fresh, scale, router, serve_out, fresh_out, scale_out, router_out, sem):
    copies = [
        pltpu.make_async_copy(scale, scale_out, sem.at[0]),
        pltpu.make_async_copy(router, router_out, sem.at[1]),
    ]
    n = ROWS // PIECES
    for k in range(PIECES):
        rows = pl.ds(k * n, n)
        copies.append(pltpu.make_async_copy(serve.at[rows], serve_out.at[rows], sem.at[2 + 2 * k]))
        copies.append(pltpu.make_async_copy(fresh.at[rows], fresh_out.at[rows], sem.at[3 + 2 * k]))
    for copy in copies:
        copy.start()
    for copy in copies:
        copy.wait()


def store(serve, fresh, scale, router):
    vmem, any_ = pl.BlockSpec(memory_space=pltpu.VMEM), pl.BlockSpec(memory_space=pl.ANY)
    return pl.pallas_call(
        store_kernel,
        out_shape=tuple(pltpu.HBM(v.shape, v.dtype) for v in (serve, fresh, scale, router)),
        in_specs=[vmem] * 4,
        out_specs=(any_,) * 4,
        scratch_shapes=[pltpu.SemaphoreType.DMA((2 + 2 * PIECES,))],
        compiler_params=pltpu.CompilerParams(vmem_limit_bytes=16 << 20),
        name="store",
    )(*(pltpu.with_memory_space_constraint(v, pltpu.VMEM) for v in (serve, fresh, scale, router)))


def body(w_down, avg_down, router_weight, router_gain):
    serve, fresh, scale, router = store(
        *gather(
            w_down.reshape(ROWS, COLS),
            avg_down.reshape(ROWS, COLS),
            router_weight.reshape(1, COLS),
            router_gain.reshape(1, COLS),
        )
    )
    return (
        serve.reshape(1, ROWS, WIDE),
        scale,
        router.reshape(NZ * NY * NC, WIDE).T,
        fresh.reshape(1, ROWS, COLS),
    )


def solution(mesh):
    placed = (P("ep", None, "fsdp"), P("ep", None, "fsdp"), P("fsdp", "ep"), P("fsdp"))
    return jax.shard_map(
        body,
        mesh=mesh,
        in_specs=placed,
        out_specs=(P("ep", None, None), P("ep", None), P(), P("ep", None, "fsdp")),
        check_vma=False,
    )
```

time: 100 us -> 64.1 us (0.64)
  Pallas kernels: 0 us -> 63.4 us
  waiting for transfers between devices: 36.8 us -> 0 us
  blocking collectives: 19.9 us -> 0 us
  between operations: 14.1 us -> 0.64 us
  starting transfers between devices: 12.1 us -> 0 us
  local copies, waits for them, and re-layouts: 9.53 us -> 0 us
  other arithmetic: 6.74 us -> 0 us
    pallas_call x0 -> x2, Pallas kernels: none -> 63.4 us  [the longest x1 59.8 us: gather(): pl.pallas_call(gather_kernel, out_shape=(pltpu.VMEM((ROWS, WIDE), BF16),...]
    all_gather x1 -> x0, waiting for transfers between devices: 25.2 us -> none  [body(): serve_down = lax.all_gather(narrow_down, 'fsdp', axis=2, tiled=True)]
    all_to_all x1 -> x0, starting transfers between devices: 12.1 us -> none  [sent_to_all(): return lax.all_to_all(copies, axis, split_axis=0, concat_axis=0, tiled=True)]
    all_to_all x1 -> x0, waiting for transfers between devices: 11.6 us -> none  [sent_to_all(): return lax.all_to_all(copies, axis, split_axis=0, concat_axis=0, tiled=True)]
    all_gather x1 -> x0, blocking collectives: 10.4 us -> none  [body(): row_router = lax.all_gather(part_router, 'fsdp', axis=0, tiled=True)]
    all_to_all x1 -> x0, blocking collectives: 9.49 us -> none  [sent_to_all(): return lax.all_to_all(copies, axis, split_axis=0, concat_axis=0, tiled=True)]
    unnamed x11 -> x0, local copies, waits for them, and re-layouts: 8.06 us -> none
    reduce_max x2 -> x0, other arithmetic: 3.18 us -> none  [the longest x1 3.15 us: body(): scale_down = of_everyone(jnp.max(jnp.abs(fresh_down), axis=2), 'fsdp')]
  transfers between devices with their start and end apart: 2 -> 0, of which waited for: 2 -> 0; matrix products, arithmetic and copies ran while one was open for 6% -> 0% of each run, Pallas kernels for 0% -> 0%
where the time goes in v1:
time: 64.1 us; the launch traced here: 64 us
  Pallas kernels  63.4 us (99%)
    pallas_call x1, Pallas kernels, gather(): pl.pallas_call(gather_kernel, out_shape=(pltpu.VMEM((ROWS, WIDE), BF16),...  59.8 us
    pallas_call x1, Pallas kernels, store(): pl.pallas_call(store_kernel, out_shape=tuple((pltpu.HBM(v.shape, v.dtype)...  3.59 us

profile of v1, /device:TPU:8, one launch (start us, length us, event | category | flops | bytes accessed | tf_op | source)
XLA Modules:
  0.0 64.0 jit_solution(18340509511423509114)
XLA Ops:
  0.6 59.8 %gather.1 = (bf16[1408,2048]{1,0:T(8,128)(2,1)S(1)}, f32[1408,512]{1,0:T(8,128)S(1)}, f32[1,1408]{1,0:T(1,128)S(1)}, bf16[8,8,2048]{2,1,0:T(8,128)(2,1)S(1)}) custom-call(f32[1408,512]{1,0:T(8,128)} %bitcast.9, f32[1408,512]{1,0:T(8,128)} %bitcast.10, f32[1,512]{1,0:T(1,128)} %bitcast.11, f32[1,512]{1,0:T(1,128)} %bitcast.12), custom_call_target="tpu_custom_call" | custom-call | tf_op jit(solution)/shard_map/gather/pallas_call | solution.py:210
  60.4 3.6 %store.1 = (bf16[1408,2048]{1,0:T(8,128)(2,1)}, f32[1408,512]{1,0:T(8,128)}, f32[1,1408]{1,0:T(1,128)}, bf16[8,8,2048]{2,1,0:T(8,128)(2,1)}) custom-call(bf16[1408,2048]{1,0:T(8,128)(2,1)S(1)} %get-tuple-element.12.serve, f32[1408,512]{1,0:T(8,128)S(1)} %get-tuple-element.13.fresh, f32[1,1408]{1,0:T(1,128)S(1)} %get-tuple-element.14.scale, ...), custom_call_target="tpu_custom_call" | custom-call | tf_op jit(solution)/shard_map/store/pallas_call | solution.py:274

commit v2 on v1

--- a/solution.py
+++ b/solution.py
@@ -23,7 +23,7 @@
     w_hbm, a_hbm, rw_hbm, gain_hbm, serve, fresh, scale, router,
     wbuf, abuf, rw, gain, m0, m1, piece, wide,
     load_sem, small_sem, m_send, m_recv, own_send, own_recv, fwd_send, fwd_recv,
-    r0_send, r0_recv, r1_send, r1_recv, r2_send, r2_recv, r3_send, r3_recv,
+    r0_send, r0_recv, r1_send, r1_recv, r2_send, r2_recv, r3_send, r3_recv, greeted,
 ):
     x, e = lax.axis_index("fsdp"), lax.axis_index("ep")
     right, far, left = lax.rem(x + 1, NX), lax.rem(x + 2, NX), lax.rem(x + 3, NX)
@@ -60,9 +60,23 @@
     lax.fori_loop(1, NB, start_load, 0)
 
     barrier = pltpu.get_barrier_semaphore()
-    peers = (*x_peers, mate, y_up, y_down, z_up, z_down)
-    for peer in peers:
+    for peer in x_peers:
         pl.semaphore_signal(barrier, inc=1, device_id=peer, device_id_type=MESH)
+    links = (
+        (c == 0, c == 1, mate),
+        (y < NY - 1, y == NY - 1, y_up),
+        (y == 0, y > 0, y_down),
+        (z < NZ - 1, z == NZ - 1, z_up),
+        (z == 0, z > 0, z_down),
+    )
+    entries, greetings = 3, 0
+    for leads, follows, peer in links:
+        entries += follows.astype(jnp.int32)
+        greetings += leads.astype(jnp.int32)
+
+        @pl.when(leads)
+        def _(peer=peer):
+            pl.semaphore_signal(barrier, inc=1, device_id=peer, device_id_type=MESH)
 
     def average(b):
         load(b, 0).wait()
@@ -82,7 +96,13 @@
     part = rw[...] * gain[...]
     for k in range(NX):
         piece[lo, x, k : k + 1, :] = part[:, k * 128 : (k + 1) * 128]
-    pl.semaphore_wait(barrier, len(peers))
+    pl.semaphore_wait(barrier, entries)
+    for _, follows, peer in links:
+
+        @pl.when(follows)
+        def _(peer=peer):
+            pl.semaphore_signal(greeted, inc=1, device_id=peer, device_id_type=MESH)
+
 
     first = [remote(m0.at[x], m0.at[x], m_send.at[0, k], m_recv.at[0, k], x_peers[k]) for k in range(3)]
     rest = [remote(m1.at[x], m1.at[x], m_send.at[1, k], m_recv.at[1, k], x_peers[k]) for k in range(3)]
@@ -143,6 +163,10 @@
 
     lax.fori_loop(1, NB, first_halves, 0)
     lax.fori_loop(1, NB, second_halves, 0)
+
+    @pl.when(greetings > 0)
+    def _():
+        pl.semaphore_wait(greeted, greetings)
 
     for copy in r0:
         copy.wait_recv()
@@ -242,6 +266,7 @@
             dma((3,)),
             dma((2, NZ // 2)),
             dma((2, NZ // 2)),
+            pltpu.SemaphoreType.REGULAR,
         ],
         compiler_params=pltpu.CompilerParams(
             collective_id=0, has_side_effects=True, vmem_limit_bytes=24 << 20

time: 64.1 us -> 60.3 us (0.941)
  Pallas kernels: 63.4 us -> 59.6 us
    pallas_call x1, Pallas kernels: 59.8 us -> 56 us  [gather(): pl.pallas_call(gather_kernel, out_shape=(pltpu.VMEM((ROWS, WIDE), BF16),...]
where the time goes in v2:
time: 60.3 us; the launch traced here: 60.2 us
  Pallas kernels  59.6 us (99%)
  between operations  0.64 us (1%)
    pallas_call x1, Pallas kernels, gather(): pl.pallas_call(gather_kernel, out_shape=(pltpu.VMEM((ROWS, WIDE), BF16),...  56 us
    pallas_call x1, Pallas kernels, store(): pl.pallas_call(store_kernel, out_shape=tuple((pltpu.HBM(v.shape, v.dtype)...  3.59 us

profile of v2, /device:TPU:8, one launch (start us, length us, event | category | flops | bytes accessed | tf_op | source)
XLA Modules:
  0.0 60.2 jit_solution(7513906489660465659)
XLA Ops:
  0.6 56.0 %gather.1 = (bf16[1408,2048]{1,0:T(8,128)(2,1)S(1)}, f32[1408,512]{1,0:T(8,128)S(1)}, f32[1,1408]{1,0:T(1,128)S(1)}, bf16[8,8,2048]{2,1,0:T(8,128)(2,1)S(1)}) custom-call(f32[1408,512]{1,0:T(8,128)} %bitcast.9, f32[1408,512]{1,0:T(8,128)} %bitcast.10, f32[1,512]{1,0:T(1,128)} %bitcast.11, f32[1,512]{1,0:T(1,128)} %bitcast.12), custom_call_target="tpu_custom_call" | custom-call | tf_op jit(solution)/shard_map/gather/pallas_call | solution.py:234
  56.7 3.6 %store.1 = (bf16[1408,2048]{1,0:T(8,128)(2,1)}, f32[1408,512]{1,0:T(8,128)}, f32[1,1408]{1,0:T(1,128)}, bf16[8,8,2048]{2,1,0:T(8,128)(2,1)}) custom-call(bf16[1408,2048]{1,0:T(8,128)(2,1)S(1)} %get-tuple-element.12.serve, f32[1408,512]{1,0:T(8,128)S(1)} %get-tuple-element.13.fresh, f32[1,1408]{1,0:T(1,128)S(1)} %get-tuple-element.14.scale, ...), custom_call_target="tpu_custom_call" | custom-call | tf_op jit(solution)/shard_map/store/pallas_call | solution.py:299

commit v3 on v2

--- a/solution.py
+++ b/solution.py
@@ -13,6 +13,8 @@
 HALF = COLS // 2
 BLK = 128
 NB = ROWS // BLK
+EARLY = (40, 24)
+NE = sum(EARLY)
 
 
 def rows_of(b):
@@ -21,8 +23,8 @@
 
 def gather_kernel(
     w_hbm, a_hbm, rw_hbm, gain_hbm, serve, fresh, scale, router,
-    wbuf, abuf, rw, gain, m0, m1, piece, wide,
-    load_sem, small_sem, m_send, m_recv, own_send, own_recv, fwd_send, fwd_recv,
+    wbuf, abuf, rw, gain, m0, m1, early, piece, wide,
+    load_sem, small_sem, m_send, m_recv, e_send, e_recv, own_send, own_recv, fwd_send, fwd_recv,
     r0_send, r0_recv, r1_send, r1_recv, r2_send, r2_recv, r3_send, r3_recv, greeted,
 ):
     x, e = lax.axis_index("fsdp"), lax.axis_index("ep")
@@ -109,7 +111,11 @@
     r0 = [remote(piece.at[lo, x], piece.at[lo, x], r0_send.at[k], r0_recv.at[k], x_peers[k]) for k in range(3)]
     for copy in first:
         copy.start()
-    for copy in r0:
+    ahead = [
+        [remote(fresh.at[rows], early.at[d, rows], e_send.at[d, k], e_recv.at[d, k], x_peers[d]) for d in range(2)]
+        for k, rows in enumerate((pl.ds(0, EARLY[0]), pl.ds(EARLY[0], EARLY[1])))
+    ]
+    for copy in (*ahead[0], *r0):
         copy.start()
 
     def maxima(b, carry):
@@ -117,52 +123,69 @@
         return carry
 
     lax.fori_loop(1, NB, maxima, 0)
-    for copy in rest:
+    for copy in (*rest, *ahead[1]):
         copy.start()
 
     mine = x * COLS
 
-    def own(b, h, d):
-        ref = serve.at[rows_of(b), pl.ds(pl.multiple_of(mine + h * HALF, HALF), HALF)]
-        return remote(ref, ref, own_send.at[d, h, b], own_recv.at[d, h, b], x_peers[d])
-
-    def forward(b, d):
-        start = (left if d == 0 else right) * COLS + d * HALF
-        ref = serve.at[rows_of(b), pl.ds(pl.multiple_of(start, HALF), HALF)]
-        return remote(ref, ref, fwd_send.at[d, b], fwd_recv.at[d, b], x_peers[d])
-
-    def narrow(b, top):
-        here = rows_of(b)
-        scale[:, pl.ds(pl.multiple_of(b * BLK, BLK), BLK)] = top
-        tall = jnp.broadcast_to(top, (BLK, BLK)).T
+    def columns(start, width):
+        return pl.ds(pl.multiple_of(start, 128), width)
+
+    def rows_in(unit):
+        if isinstance(unit, int) and unit < 2:
+            return (pl.ds(0, NE), pl.ds(NE, BLK - NE))[unit]
+        return rows_of(unit - 1)
+
+    def own(unit, h, d):
+        ref = serve.at[rows_in(unit), columns(mine + h * HALF, HALF)]
+        return remote(ref, ref, own_send.at[d, h, unit - 1], own_recv.at[d, h, unit - 1], x_peers[d])
+
+    def forward(unit, d):
+        ref = serve.at[rows_in(unit), columns((left if d == 0 else right) * COLS + d * HALF, HALF)]
+        return remote(ref, ref, fwd_send.at[d, unit], fwd_recv.at[d, unit], x_peers[d])
+
+    def tall(top):
+        return jnp.broadcast_to(top, (BLK, BLK)).T
+
+    def narrow(src, here, start, scales):
         for k in range(COLS // 128):
-            value = fresh[here, pl.ds(k * 128, 128)] / tall
-            serve[here, pl.ds(pl.multiple_of(mine + k * 128, 128), 128)] = value.astype(BF16)
+            value = src[here, pl.ds(k * 128, 128)] / scales
+            serve[here, columns(start + k * 128, 128)] = value.astype(BF16)
 
     for copy in first:
         copy.wait_recv()
-    narrow(0, jnp.maximum(jnp.maximum(m0[0], m0[1]), jnp.maximum(m0[2], m0[3])))
-    own(0, 0, 0).start()
-    own(0, 1, 1).start()
-    own(0, 1, 0).start()
-    own(0, 0, 1).start()
+    top = jnp.maximum(jnp.maximum(m0[0], m0[1]), jnp.maximum(m0[2], m0[3]))
+    scale[:, 0:BLK] = top
+    scales = tall(top)
+    narrow(fresh, rows_in(1), mine, scales[NE:])
+    for h, d in ((0, 0), (1, 1), (1, 0), (0, 1)):
+        own(1, h, d).start()
+    narrow(fresh, rows_in(0), mine, scales[:NE])
     for copy in rest:
         copy.wait_recv()
 
     def first_halves(b, carry):
         at = pl.ds(b - 1, 1)
-        narrow(b, jnp.maximum(jnp.maximum(m1[0, at], m1[1, at]), jnp.maximum(m1[2, at], m1[3, at])))
-        own(b, 0, 0).start()
-        own(b, 1, 1).start()
+        top = jnp.maximum(jnp.maximum(m1[0, at], m1[1, at]), jnp.maximum(m1[2, at], m1[3, at]))
+        scale[:, columns(b * BLK, BLK)] = top
+        narrow(fresh, rows_of(b), mine, tall(top))
+        own(b + 1, 0, 0).start()
+        own(b + 1, 1, 1).start()
         return carry
 
     def second_halves(b, carry):
-        own(b, 1, 0).start()
-        own(b, 0, 1).start()
+        own(b + 1, 1, 0).start()
+        own(b + 1, 0, 1).start()
         return carry
 
     lax.fori_loop(1, NB, first_halves, 0)
     lax.fori_loop(1, NB, second_halves, 0)
+
+    scales = tall(scale[:, 0:BLK])
+    for d, peer in ((0, left), (1, right)):
+        ahead[0][d].wait_recv()
+        ahead[1][d].wait_recv()
+        narrow(early.at[d], rows_in(0), peer * COLS, scales[:NE])
 
     @pl.when(greetings > 0)
     def _():
@@ -205,27 +228,34 @@
             if step == k:
                 copy.wait_recv()
 
-    def pass_on(b, carry):
-        own(b, 0, 0).wait_recv()
-        forward(b, 0).start()
-        own(b, 1, 1).wait_recv()
-        forward(b, 1).start()
-        return carry
-
-    lax.fori_loop(0, NB, pass_on, 0)
-
-    def finish(b, carry):
-        own(b, 1, 0).wait_recv()
-        own(b, 0, 1).wait_recv()
+    def pass_on(unit, carry=0):
+        own(unit, 0, 0).wait_recv()
+        forward(unit, 0).start()
+        own(unit, 1, 1).wait_recv()
+        forward(unit, 1).start()
+        return carry
+
+    forward(0, 0).start()
+    forward(0, 1).start()
+    pass_on(1)
+    lax.fori_loop(2, NB + 1, pass_on, 0)
+
+    def finish(unit, carry=0):
+        own(unit, 1, 0).wait_recv()
+        own(unit, 0, 1).wait_recv()
         for d in range(2):
-            forward(b, d).wait_recv()
+            forward(unit, d).wait_recv()
             for h in range(2):
-                own(b, h, d).wait_send()
-            forward(b, d).wait_send()
-        return carry
-
-    lax.fori_loop(0, NB, finish, 0)
-    for copy in (*first, *rest, *r0, r1, *r2, *[step[2] for step in r3]):
+                own(unit, h, d).wait_send()
+            forward(unit, d).wait_send()
+        return carry
+
+    for d in range(2):
+        forward(0, d).wait_recv()
+        forward(0, d).wait_send()
+    finish(1)
+    lax.fori_loop(2, NB + 1, finish, 0)
+    for copy in (*first, *rest, *ahead[0], *ahead[1], *r0, r1, *r2, *[step[2] for step in r3]):
         copy.wait_send()
 
 
@@ -248,16 +278,19 @@
             pltpu.VMEM((1, COLS), F32),
             pltpu.VMEM((NX, 1, BLK), F32),
             pltpu.VMEM((NX, NB - 1, BLK), F32),
+            pltpu.VMEM((2, NE, COLS), F32),
             pltpu.VMEM((NY * NC, NX, NX, 128), F32),
             pltpu.VMEM((NY * NC, WIDE), F32),
             dma((2, NB)),
             dma((2,)),
             dma((2, 3)),
             dma((2, 3)),
+            dma((2, 2)),
+            dma((2, 2)),
             dma((2, 2, NB)),
             dma((2, 2, NB)),
-            dma((2, NB)),
-            dma((2, NB)),
+            dma((2, NB + 1)),
+            dma((2, NB + 1)),
             dma((3,)),
             dma((3,)),
             dma,

time: 60.3 us -> 59.9 us (level)
  no operation moved by 1% of the time
where the time goes in v3:
time: 59.9 us; the launch traced here: 59.8 us
  Pallas kernels  59.2 us (99%)
  between operations  0.64 us (1%)
    pallas_call x1, Pallas kernels, gather(): pl.pallas_call(gather_kernel, out_shape=(pltpu.VMEM((ROWS, WIDE), BF16),...  55.6 us
    pallas_call x1, Pallas kernels, store(): pl.pallas_call(store_kernel, out_shape=tuple((pltpu.HBM(v.shape, v.dtype)...  3.59 us

profile of v3, /device:TPU:8, one launch (start us, length us, event | category | flops | bytes accessed | tf_op | source)
XLA Modules:
  0.0 59.8 jit_solution(9229843262735415327)
XLA Ops:
  0.6 55.6 %gather.1 = (bf16[1408,2048]{1,0:T(8,128)(2,1)S(1)}, f32[1408,512]{1,0:T(8,128)S(1)}, f32[1,1408]{1,0:T(1,128)S(1)}, bf16[8,8,2048]{2,1,0:T(8,128)(2,1)S(1)}) custom-call(f32[1408,512]{1,0:T(8,128)} %bitcast.9, f32[1408,512]{1,0:T(8,128)} %bitcast.10, f32[1,512]{1,0:T(1,128)} %bitcast.11, f32[1,512]{1,0:T(1,128)} %bitcast.12), custom_call_target="tpu_custom_call" | custom-call | tf_op jit(solution)/shard_map/gather/pallas_call | solution.py:264
  56.2 3.6 %store.1 = (bf16[1408,2048]{1,0:T(8,128)(2,1)}, f32[1408,512]{1,0:T(8,128)}, f32[1,1408]{1,0:T(1,128)}, bf16[8,8,2048]{2,1,0:T(8,128)(2,1)}) custom-call(bf16[1408,2048]{1,0:T(8,128)(2,1)S(1)} %get-tuple-element.12.serve, f32[1408,512]{1,0:T(8,128)S(1)} %get-tuple-element.13.fresh, f32[1,1408]{1,0:T(1,128)S(1)} %get-tuple-element.14.scale, ...), custom_call_target="tpu_custom_call" | custom-call | tf_op jit(solution)/shard_map/store/pallas_call | solution.py:332

commit v4 on v0

v4 whole, which is shorter than its diff:
```python
import jax
import jax.numpy as jnp
from jax import lax
from jax.experimental import pallas as pl
from jax.experimental.pallas import tpu as pltpu
from jax.sharding import PartitionSpec as P

MESH = pl.DeviceIdType.MESH
F32, BF16 = jnp.float32, jnp.bfloat16
NX, NY, NZ, NC = 4, 4, 8, 2
ROWS, COLS = 1408, 512
WIDE = NX * COLS
HALF = COLS // 2
BLK = 128
NB = ROWS // BLK
EARLY = (48, 16)
NE = sum(EARLY)


LOADS = (0, 256, 768, 1408)


def gather_kernel(
    w_hbm, a_hbm, rw_hbm, gain_hbm, serve, fresh, scale, router,
    buf, small, m0, m1, early, piece, wide,
    load_sem, small_sem, m_send, m_recv, e_send, e_recv, own_send, keep_recv, pass_recv, fwd_send, fwd_recv,
    r0_send, r0_recv, r12_send, r1_recv, r2_recv, r3_send, r3_recv, greeted,
):
    x, e = lax.axis_index("fsdp"), lax.axis_index("ep")
    right, far, left = lax.rem(x + 1, NX), lax.rem(x + 2, NX), lax.rem(x + 3, NX)
    lo = lax.rem(e, NY * NC)
    z, y, c = e // (NY * NC), lo // NC, lax.rem(lo, NC)
    x_peers = ({"fsdp": right}, {"fsdp": left}, {"fsdp": far})
    mate = {"ep": e + 1 - 2 * c}
    y_up = {"ep": z * (NY * NC) + lax.rem(y + 1, NY) * NC + c}
    y_down = {"ep": z * (NY * NC) + lax.rem(y + NY - 1, NY) * NC + c}
    z_up = {"ep": lax.rem(z + 1, NZ) * (NY * NC) + lo}
    z_down = {"ep": lax.rem(z + NZ - 1, NZ) * (NY * NC) + lo}

    barrier = pltpu.get_barrier_semaphore()
    for peer in (x_peers[2], x_peers[0], x_peers[1]):
        pl.semaphore_signal(barrier, inc=1, device_id=peer, device_id_type=MESH)

    def load(part, k):
        rows = pl.ds(LOADS[part], LOADS[part + 1] - LOADS[part])
        return pltpu.make_async_copy((w_hbm, a_hbm)[k].at[rows], buf.at[k, rows], load_sem.at[part])

    def wait_for(ref, sem):
        pltpu.make_async_copy(ref, ref, sem).wait()

    def loaded(part):
        wait_for(buf.at[:, pl.ds(LOADS[part], LOADS[part + 1] - LOADS[part])], load_sem.at[part])

    def remote(src, dst, send, recv, peer):
        return pltpu.make_async_remote_copy(
            src_ref=src, dst_ref=dst, send_sem=send, recv_sem=recv, device_id=peer, device_id_type=MESH
        )

    for part in range(len(LOADS) - 1):
        load(part, 0).start()
        load(part, 1).start()
        if part == 0:
            pltpu.make_async_copy(rw_hbm, small.at[0], small_sem).start()
            pltpu.make_async_copy(gain_hbm, small.at[1], small_sem).start()

    links = (
        (c == 1, c == 0, mate),
        (y < NY - 1, y == NY - 1, y_up),
        (y == 0, y > 0, y_down),
        (z < NZ - 1, z == NZ - 1, z_up),
        (z == 0, z > 0, z_down),
    )
    entries, greetings = 3, 0
    for leads, follows, peer in links:
        entries += follows.astype(jnp.int32)
        greetings += leads.astype(jnp.int32)

        @pl.when(leads)
        def _(peer=peer):
            pl.semaphore_signal(barrier, inc=1, device_id=peer, device_id_type=MESH)

    def rows_of(b):
        return pl.ds(pl.multiple_of(b * BLK, BLK), BLK)

    def columns(start, width):
        return pl.ds(pl.multiple_of(start, 128), width)

    def average(b):
        here = rows_of(b)
        top = None
        for k in range(COLS // 128):
            lanes = pl.ds(k * 128, 128)
            value = 0.5 * buf[1, here, lanes] + 0.5 * buf[0, here, lanes]
            fresh[here, lanes] = value
            top = jnp.abs(value) if top is None else jnp.maximum(top, jnp.abs(value))
        return jnp.max(top.T, axis=0, keepdims=True)

    loaded(0)
    for b in range(2):
        m0[x, b : b + 1, :] = average(b)
    pl.semaphore_wait(barrier, entries)

    for k in (2, 0, 1):
        remote(m0.at[x], m0.at[x], m_send.at[0], m_recv.at[0], x_peers[k]).start()
    ahead = (pl.ds(0, EARLY[0]), pl.ds(EARLY[0], EARLY[1]))
    for d in range(2):
        remote(fresh.at[ahead[0]], early.at[d, ahead[0]], e_send, e_recv, x_peers[d]).start()
    wait_for(small, small_sem)
    part = small[0] * small[1]
    for k in range(NX):
        piece[lo, x, k : k + 1, :] = part[:, k * 128 : (k + 1) * 128]
    for k in range(3):
        remote(piece.at[lo, x], piece.at[lo, x], r0_send, r0_recv, x_peers[k]).start()
    for _, follows, peer in links:

        @pl.when(follows)
        def _(peer=peer):
            pl.semaphore_signal(greeted, inc=1, device_id=peer, device_id_type=MESH)

    def maxima(b, carry):
        m1[x, pl.ds(b - 2, 1), :] = average(b)
        return carry

    for part in range(1, len(LOADS) - 1):
        loaded(part)
        lax.fori_loop(LOADS[part] // BLK, LOADS[part + 1] // BLK, maxima, 0)
    for k in (2, 0, 1):
        remote(m1.at[x], m1.at[x], m_send.at[1], m_recv.at[1], x_peers[k]).start()
    for d in range(2):
        remote(fresh.at[ahead[1]], early.at[d, ahead[1]], e_send, e_recv, x_peers[d]).start()

    mine = x * COLS

    def tall(top):
        return jnp.broadcast_to(top, (BLK, BLK)).T

    def narrow(src, here, start, scales):
        for k in range(COLS // 128):
            value = src[here, pl.ds(k * 128, 128)] / scales
            serve[here, columns(start + k * 128, 128)] = value.astype(BF16)

    def own(rows, h, d):
        ref = serve.at[rows, columns(mine + h * HALF, HALF)]
        return remote(ref, ref, own_send, pass_recv.at[d] if h == d else keep_recv, x_peers[d])

    def forward(d):
        ref = serve.at[:, columns((left if d == 0 else right) * COLS + d * HALF, HALF)]
        return remote(ref, ref, fwd_send, fwd_recv, x_peers[d])

    wait_for(m0.at[pl.ds(0, 3)], m_recv.at[0])
    top = jnp.maximum(jnp.maximum(m0[0], m0[1]), jnp.maximum(m0[2], m0[3]))
    scale[:, 0:BLK] = top[0:1]
    scale[:, BLK : 2 * BLK] = top[1:2]
    scales = tall(top[0:1])
    narrow(fresh, pl.ds(NE, BLK - NE), mine, scales[NE:])
    narrow(fresh, rows_of(1), mine, tall(top[1:2]))
    for h, d in ((0, 0), (1, 1), (1, 0), (0, 1)):
        own(pl.ds(NE, 2 * BLK - NE), h, d).start()
    narrow(fresh, pl.ds(0, NE), mine, scales[:NE])
    wait_for(m1.at[pl.ds(0, 3)], m_recv.at[1])

    def narrowed(b, carry):
        at = pl.ds(b - 2, 1)
        top = jnp.maximum(jnp.maximum(m1[0, at], m1[1, at]), jnp.maximum(m1[2, at], m1[3, at]))
        scale[:, columns(b * BLK, BLK)] = top
        narrow(fresh, rows_of(b), mine, tall(top))
        return carry

    lax.fori_loop(2, NB, narrowed, 0)
    for h, d in ((0, 0), (1, 1), (1, 0), (0, 1)):
        own(pl.ds(2 * BLK, ROWS - 2 * BLK), h, d).start()

    wait_for(early, e_recv)
    scales = tall(scale[:, 0:BLK])
    for d, peer in ((0, left), (1, right)):
        narrow(early.at[d], pl.ds(0, NE), peer * COLS, scales[:NE])

    @pl.when(greetings > 0)
    def _():
        pl.semaphore_wait(greeted, greetings)

    wait_for(piece.at[lo, pl.ds(0, 3)], r0_recv)
    remote(piece.at[lo], piece.at[lo], r12_send, r1_recv, mate).start()
    chip = piece.at[pl.ds(y * NC, NC)]
    below = piece.at[pl.ds(lax.rem(y + NY - 1, NY) * NC, NC)]
    wait_for(piece.at[0], r1_recv)
    remote(chip, chip, r12_send, r2_recv.at[0], y_up).start()
    remote(chip, chip, r12_send, r2_recv.at[1], y_down).start()
    wait_for(chip, r2_recv.at[0])
    remote(below, below, r12_send, r2_recv.at[1], y_up).start()
    wait_for(piece.at[pl.ds(0, 2 * NC)], r2_recv.at[1])
    for i in range(NY * NC):
        for k in range(WIDE // 128):
            wide[i : i + 1, k * 128 : (k + 1) * 128] = piece[i, k // 4, k % 4 : k % 4 + 1, :]
    router[z] = wide[...].astype(BF16)

    def z_step(k):
        for d, peer in ((0, z_up), (1, z_down)):
            if d == 0 or k < NZ // 2 - 1:
                plane = router.at[lax.rem(z + (NZ - k if d == 0 else k), NZ)]
                remote(plane, plane, r3_send, r3_recv.at[k], peer).start()

    def z_arrived(k):
        wait_for(router.at[pl.ds(0, 2 if k < NZ // 2 - 1 else 1)], r3_recv.at[k])

    z_step(0)
    for d in range(2):
        wait_for(serve.at[pl.ds(NE, ROWS - NE), columns(0, HALF)], pass_recv.at[d])
        forward(d).start()
    for k in range(1, NZ // 2):
        z_arrived(k - 1)
        z_step(k)
    z_arrived(NZ // 2 - 1)

    wait_for(early, e_send)
    for k, m in enumerate((m0, m1)):
        wait_for(m.at[pl.ds(0, 3)], m_send.at[k])
    wait_for(piece.at[0, pl.ds(0, 3)], r0_send)
    wait_for(piece.at[pl.ds(0, 1 + 3 * NC)], r12_send)
    wait_for(router.at[pl.ds(0, NZ - 1)], r3_send)
    wait_for(serve.at[pl.ds(NE, ROWS - NE), columns(0, COLS)], keep_recv)
    wait_for(serve.at[pl.ds(NE, ROWS - NE), columns(0, 2 * COLS)], own_send)
    wait_for(serve.at[:, columns(0, COLS)], fwd_send)
    wait_for(serve.at[:, columns(0, COLS)], fwd_recv)


def gather(w_down, avg_down, rw, gain):
    dma, any_, vmem = pltpu.SemaphoreType.DMA, pl.BlockSpec(memory_space=pl.ANY), pl.BlockSpec(memory_space=pltpu.VMEM)
    return pl.pallas_call(
        gather_kernel,
        out_shape=(
            pltpu.VMEM((ROWS, WIDE), BF16),
            pltpu.VMEM((ROWS, COLS), F32),
            pltpu.VMEM((1, ROWS), F32),
            pltpu.VMEM((NZ, NY * NC, WIDE), BF16),
        ),
        in_specs=[any_] * 4,
        out_specs=(vmem, vmem, vmem, vmem),
        scratch_shapes=[
            pltpu.VMEM((2, ROWS, COLS), F32),
            pltpu.VMEM((2, 1, COLS), F32),
            pltpu.VMEM((NX, 2, BLK), F32),
            pltpu.VMEM((NX, NB - 2, BLK), F32),
            pltpu.VMEM((2, NE, COLS), F32),
            pltpu.VMEM((NY * NC, NX, NX, 128), F32),
            pltpu.VMEM((NY * NC, WIDE), F32),
            dma((len(LOADS) - 1,)),
            dma,
            dma((2,)),
            dma((2,)),
            dma,
            dma,
            dma,
            dma,
            dma((2,)),
            dma,
            dma,
            dma,
            dma,
            dma,
            dma,
            dma((2,)),
            dma,
            dma((NZ // 2,)),
            pltpu.SemaphoreType.REGULAR,
        ],
        compiler_params=pltpu.CompilerParams(
            collective_id=0, has_side_effects=True, vmem_limit_bytes=24 << 20
        ),
        name="gather",
    )(*(pltpu.with_memory_space_constraint(v, pltpu.HBM) for v in (w_down, avg_down, rw, gain)))


def store_kernel(serve, fresh, scale, router, serve_out, fresh_out, scale_out, router_out, sem):
    pairs = ((serve, serve_out), (fresh, fresh_out), (router, router_out), (scale, scale_out))
    copies = [pltpu.make_async_copy(src, dst, sem.at[k]) for k, (src, dst) in enumerate(pairs)]
    for copy in copies:
        copy.start()
    for copy in copies:
        copy.wait()


def store(serve, fresh, scale, router):
    vmem, any_ = pl.BlockSpec(memory_space=pltpu.VMEM), pl.BlockSpec(memory_space=pl.ANY)
    return pl.pallas_call(
        store_kernel,
        out_shape=tuple(pltpu.HBM(v.shape, v.dtype) for v in (serve, fresh, scale, router)),
        in_specs=[vmem] * 4,
        out_specs=(any_,) * 4,
        scratch_shapes=[pltpu.SemaphoreType.DMA((4,))],
        compiler_params=pltpu.CompilerParams(vmem_limit_bytes=16 << 20),
        name="store",
    )(*(pltpu.with_memory_space_constraint(v, pltpu.VMEM) for v in (serve, fresh, scale, router)))


def body(w_down, avg_down, router_weight, router_gain):
    serve, fresh, scale, router = store(
        *gather(
            w_down.reshape(ROWS, COLS),
            avg_down.reshape(ROWS, COLS),
            router_weight.reshape(1, COLS),
            router_gain.reshape(1, COLS),
        )
    )
    return (
        serve.reshape(1, ROWS, WIDE),
        scale,
        router.reshape(NZ * NY * NC, WIDE).T,
        fresh.reshape(1, ROWS, COLS),
    )


def solution(mesh):
    placed = (P("ep", None, "fsdp"), P("ep", None, "fsdp"), P("fsdp", "ep"), P("fsdp"))
    return jax.shard_map(
        body,
        mesh=mesh,
        in_specs=placed,
        out_specs=(P("ep", None, None), P("ep", None), P(), P("ep", None, "fsdp")),
        check_vma=False,
    )
```

time: 100 us -> 58.1 us (0.58)
  Pallas kernels: 0 us -> 56.9 us
  waiting for transfers between devices: 36.8 us -> 0 us
  blocking collectives: 19.9 us -> 0 us
  between operations: 14.1 us -> 0.64 us
  starting transfers between devices: 12.1 us -> 0 us
  local copies, waits for them, and re-layouts: 9.53 us -> 0 us
  other arithmetic: 6.74 us -> 0 us
    pallas_call x0 -> x2, Pallas kernels: none -> 56.9 us  [the longest x1 53.4 us: gather(): pl.pallas_call(gather_kernel, out_shape=(pltpu.VMEM((ROWS, WIDE), BF16),...]
    all_gather x1 -> x0, waiting for transfers between devices: 25.2 us -> none  [body(): serve_down = lax.all_gather(narrow_down, 'fsdp', axis=2, tiled=True)]
    all_to_all x1 -> x0, starting transfers between devices: 12.1 us -> none  [sent_to_all(): return lax.all_to_all(copies, axis, split_axis=0, concat_axis=0, tiled=True)]
    all_to_all x1 -> x0, waiting for transfers between devices: 11.6 us -> none  [sent_to_all(): return lax.all_to_all(copies, axis, split_axis=0, concat_axis=0, tiled=True)]
    all_gather x1 -> x0, blocking collectives: 10.4 us -> none  [body(): row_router = lax.all_gather(part_router, 'fsdp', axis=0, tiled=True)]
    all_to_all x1 -> x0, blocking collectives: 9.49 us -> none  [sent_to_all(): return lax.all_to_all(copies, axis, split_axis=0, concat_axis=0, tiled=True)]
    unnamed x11 -> x0, local copies, waits for them, and re-layouts: 8.06 us -> none
    reduce_max x2 -> x0, other arithmetic: 3.18 us -> none  [the longest x1 3.15 us: body(): scale_down = of_everyone(jnp.max(jnp.abs(fresh_down), axis=2), 'fsdp')]
  transfers between devices with their start and end apart: 2 -> 0, of which waited for: 2 -> 0; matrix products, arithmetic and copies ran while one was open for 6% -> 0% of each run, Pallas kernels for 0% -> 0%
where the time goes in v4:
time: 58.1 us; the launch traced here: 57.5 us
  Pallas kernels  56.9 us (98%)
  between operations  0.64 us (1%)
    pallas_call x1, Pallas kernels, gather(): pl.pallas_call(gather_kernel, out_shape=(pltpu.VMEM((ROWS, WIDE), BF16),...  53.4 us
    pallas_call x1, Pallas kernels, store(): pl.pallas_call(store_kernel, out_shape=tuple((pltpu.HBM(v.shape, v.dtype)...  3.52 us

profile of v4, /device:TPU:8, one launch (start us, length us, event | category | flops | bytes accessed | tf_op | source)
XLA Modules:
  0.0 57.5 jit_solution(12325256129474728898)
XLA Ops:
  0.6 53.4 %gather.1 = (bf16[1408,2048]{1,0:T(8,128)(2,1)S(1)}, f32[1408,512]{1,0:T(8,128)S(1)}, f32[1,1408]{1,0:T(1,128)S(1)}, bf16[8,8,2048]{2,1,0:T(8,128)(2,1)S(1)}) custom-call(f32[1408,512]{1,0:T(8,128)} %bitcast.9, f32[1408,512]{1,0:T(8,128)} %bitcast.10, f32[1,512]{1,0:T(1,128)} %bitcast.11, f32[1,512]{1,0:T(1,128)} %bitcast.12), custom_call_target="tpu_custom_call" | custom-call | tf_op jit(solution)/shard_map/gather/pallas_call | solution.py:229
  54.0 3.5 %store.1 = (bf16[1408,2048]{1,0:T(8,128)(2,1)}, f32[1408,512]{1,0:T(8,128)}, f32[1,1408]{1,0:T(1,128)}, bf16[8,8,2048]{2,1,0:T(8,128)(2,1)}) custom-call(bf16[1408,2048]{1,0:T(8,128)(2,1)S(1)} %get-tuple-element.12.serve, f32[1408,512]{1,0:T(8,128)S(1)} %get-tuple-element.13.fresh, f32[1,1408]{1,0:T(1,128)S(1)} %get-tuple-element.14.scale, ...), custom_call_target="tpu_custom_call" | custom-call | tf_op jit(solution)/shard_map/store/pallas_call | solution.py:285

commit v5 on v4

--- a/solution.py
+++ b/solution.py
@@ -13,10 +13,11 @@
 HALF = COLS // 2
 BLK = 128
 NB = ROWS // BLK
-EARLY = (48, 16)
-NE = sum(EARLY)
-
-
+NE = 48
+
+
+RS = (1232, 800)
+REST = ROWS - min(RS)
 LOADS = (0, 256, 768, 1408)
 
 
@@ -102,9 +103,8 @@
 
     for k in (2, 0, 1):
         remote(m0.at[x], m0.at[x], m_send.at[0], m_recv.at[0], x_peers[k]).start()
-    ahead = (pl.ds(0, EARLY[0]), pl.ds(EARLY[0], EARLY[1]))
     for d in range(2):
-        remote(fresh.at[ahead[0]], early.at[d, ahead[0]], e_send, e_recv, x_peers[d]).start()
+        remote(fresh.at[pl.ds(0, NE)], early.at[d], e_send, e_recv, x_peers[d]).start()
     wait_for(small, small_sem)
     part = small[0] * small[1]
     for k in range(NX):
@@ -126,8 +126,6 @@
         lax.fori_loop(LOADS[part] // BLK, LOADS[part + 1] // BLK, maxima, 0)
     for k in (2, 0, 1):
         remote(m1.at[x], m1.at[x], m_send.at[1], m_recv.at[1], x_peers[k]).start()
-    for d in range(2):
-        remote(fresh.at[ahead[1]], early.at[d, ahead[1]], e_send, e_recv, x_peers[d]).start()
 
     mine = x * COLS
 
@@ -143,9 +141,25 @@
         ref = serve.at[rows, columns(mine + h * HALF, HALF)]
         return remote(ref, ref, own_send, pass_recv.at[d] if h == d else keep_recv, x_peers[d])
 
-    def forward(d):
-        ref = serve.at[:, columns((left if d == 0 else right) * COLS + d * HALF, HALF)]
+    def forward(n, d):
+        ref = serve.at[pl.ds(0, n), columns((left if d == 0 else right) * COLS + d * HALF, HALF)]
         return remote(ref, ref, fwd_send, fwd_recv, x_peers[d])
+
+    def by_core(do):
+        for core, n in enumerate(RS):
+            pl.when(c == core)(lambda n=n: do(n))
+
+    chip = piece.at[pl.ds(y * NC, NC)]
+    below = piece.at[pl.ds(lax.rem(y + NY - 1, NY) * NC, NC)]
+
+    def z_step(k):
+        for d, peer in ((0, z_up), (1, z_down)):
+            if d == 0 or k < NZ // 2 - 1:
+                plane = router.at[lax.rem(z + (NZ - k if d == 0 else k), NZ)]
+                remote(plane, plane, r3_send, r3_recv.at[k], peer).start()
+
+    def z_arrived(k):
+        wait_for(router.at[pl.ds(0, 2 if k < NZ // 2 - 1 else 1)], r3_recv.at[k])
 
     wait_for(m0.at[pl.ds(0, 3)], m_recv.at[0])
     top = jnp.maximum(jnp.maximum(m0[0], m0[1]), jnp.maximum(m0[2], m0[3]))
@@ -157,6 +171,13 @@
     for h, d in ((0, 0), (1, 1), (1, 0), (0, 1)):
         own(pl.ds(NE, 2 * BLK - NE), h, d).start()
     narrow(fresh, pl.ds(0, NE), mine, scales[:NE])
+
+    @pl.when(greetings > 0)
+    def _():
+        pl.semaphore_wait(greeted, greetings)
+
+    wait_for(piece.at[lo, pl.ds(0, 3)], r0_recv)
+    remote(piece.at[lo], piece.at[lo], r12_send, r1_recv, mate).start()
     wait_for(m1.at[pl.ds(0, 3)], m_recv.at[1])
 
     def narrowed(b, carry):
@@ -167,25 +188,21 @@
         return carry
 
     lax.fori_loop(2, NB, narrowed, 0)
-    for h, d in ((0, 0), (1, 1), (1, 0), (0, 1)):
-        own(pl.ds(2 * BLK, ROWS - 2 * BLK), h, d).start()
+
+    @by_core
+    def _(n):
+        for h, d in ((0, 0), (1, 1), (1, 0), (0, 1)):
+            own(pl.ds(2 * BLK, n - 2 * BLK), h, d).start()
+
+    wait_for(piece.at[0], r1_recv)
+    remote(chip, chip, r12_send, r2_recv.at[0], y_up).start()
+    remote(chip, chip, r12_send, r2_recv.at[1], y_down).start()
 
     wait_for(early, e_recv)
     scales = tall(scale[:, 0:BLK])
     for d, peer in ((0, left), (1, right)):
         narrow(early.at[d], pl.ds(0, NE), peer * COLS, scales[:NE])
 
-    @pl.when(greetings > 0)
-    def _():
-        pl.semaphore_wait(greeted, greetings)
-
-    wait_for(piece.at[lo, pl.ds(0, 3)], r0_recv)
-    remote(piece.at[lo], piece.at[lo], r12_send, r1_recv, mate).start()
-    chip = piece.at[pl.ds(y * NC, NC)]
-    below = piece.at[pl.ds(lax.rem(y + NY - 1, NY) * NC, NC)]
-    wait_for(piece.at[0], r1_recv)
-    remote(chip, chip, r12_send, r2_recv.at[0], y_up).start()
-    remote(chip, chip, r12_send, r2_recv.at[1], y_down).start()
     wait_for(chip, r2_recv.at[0])
     remote(below, below, r12_send, r2_recv.at[1], y_up).start()
     wait_for(piece.at[pl.ds(0, 2 * NC)], r2_recv.at[1])
@@ -193,21 +210,18 @@
         for k in range(WIDE // 128):
             wide[i : i + 1, k * 128 : (k + 1) * 128] = piece[i, k // 4, k % 4 : k % 4 + 1, :]
     router[z] = wide[...].astype(BF16)
-
-    def z_step(k):
-        for d, peer in ((0, z_up), (1, z_down)):
-            if d == 0 or k < NZ // 2 - 1:
-                plane = router.at[lax.rem(z + (NZ - k if d == 0 else k), NZ)]
-                remote(plane, plane, r3_send, r3_recv.at[k], peer).start()
-
-    def z_arrived(k):
-        wait_for(router.at[pl.ds(0, 2 if k < NZ // 2 - 1 else 1)], r3_recv.at[k])
-
     z_step(0)
-    for d in range(2):
-        wait_for(serve.at[pl.ds(NE, ROWS - NE), columns(0, HALF)], pass_recv.at[d])
-        forward(d).start()
-    for k in range(1, NZ // 2):
+    if NZ > 2:
+        z_arrived(0)
+        z_step(1)
+
+    @by_core
+    def _(n):
+        for d in range(2):
+            wait_for(serve.at[pl.ds(NE, n - NE), columns(0, HALF)], pass_recv.at[d])
+            forward(n, d).start()
+
+    for k in range(2, NZ // 2):
         z_arrived(k - 1)
         z_step(k)
     z_arrived(NZ // 2 - 1)
@@ -218,10 +232,53 @@
     wait_for(piece.at[0, pl.ds(0, 3)], r0_send)
     wait_for(piece.at[pl.ds(0, 1 + 3 * NC)], r12_send)
     wait_for(router.at[pl.ds(0, NZ - 1)], r3_send)
-    wait_for(serve.at[pl.ds(NE, ROWS - NE), columns(0, COLS)], keep_recv)
-    wait_for(serve.at[pl.ds(NE, ROWS - NE), columns(0, 2 * COLS)], own_send)
-    wait_for(serve.at[:, columns(0, COLS)], fwd_send)
-    wait_for(serve.at[:, columns(0, COLS)], fwd_recv)
+
+    @by_core
+    def _(n):
+        wait_for(serve.at[pl.ds(NE, n - NE), columns(0, COLS)], keep_recv)
+        wait_for(serve.at[pl.ds(NE, n - NE), columns(0, 2 * COLS)], own_send)
+        wait_for(serve.at[pl.ds(0, n), columns(0, COLS)], fwd_send)
+        wait_for(serve.at[pl.ds(0, n), columns(0, COLS)], fwd_recv)
+
+
+def rest_kernel(serve, stored, rest, own_send, keep_recv, pass_recv, fwd_send, fwd_recv):
+    x, c = lax.axis_index("fsdp"), lax.rem(lax.axis_index("ep"), NC)
+    right, left = lax.rem(x + 1, NX), lax.rem(x + 3, NX)
+    peers = ({"fsdp": right}, {"fsdp": left})
+    barrier = pltpu.get_barrier_semaphore()
+    for peer in peers:
+        pl.semaphore_signal(barrier, inc=1, device_id=peer, device_id_type=MESH)
+    pl.semaphore_wait(barrier, 2)
+
+    def columns(start, width):
+        return pl.ds(pl.multiple_of(start, 128), width)
+
+    def wait_for(n, width, sem):
+        ref = rest.at[pl.ds(0, n), columns(0, width)]
+        pltpu.make_async_copy(ref, ref, sem).wait()
+
+    def remote(src, dst, send, recv, d):
+        return pltpu.make_async_remote_copy(
+            src_ref=src, dst_ref=dst, send_sem=send, recv_sem=recv, device_id=peers[d], device_id_type=MESH
+        )
+
+    def gather_rest(first):
+        n = ROWS - first
+        for h, d in ((0, 0), (1, 1), (1, 0), (0, 1)):
+            lanes = columns(x * COLS + h * HALF, HALF)
+            src, dst = serve.at[pl.ds(first, n), lanes], rest.at[pl.ds(0, n), lanes]
+            remote(src, dst, own_send, pass_recv.at[d] if h == d else keep_recv, d).start()
+        for d, source in ((0, left), (1, right)):
+            wait_for(n, HALF, pass_recv.at[d])
+            ref = rest.at[pl.ds(0, n), columns(source * COLS + d * HALF, HALF)]
+            remote(ref, ref, fwd_send, fwd_recv, d).start()
+        wait_for(n, 2 * HALF, keep_recv)
+        wait_for(n, 4 * HALF, own_send)
+        wait_for(n, 2 * HALF, fwd_send)
+        wait_for(n, 2 * HALF, fwd_recv)
+
+    for core, first in enumerate(RS):
+        pl.when(c == core)(lambda first=first: gather_rest(first))
 
 
 def gather(w_down, avg_down, rw, gain):
@@ -271,37 +328,98 @@
     )(*(pltpu.with_memory_space_constraint(v, pltpu.HBM) for v in (w_down, avg_down, rw, gain)))
 
 
-def store_kernel(serve, fresh, scale, router, serve_out, fresh_out, scale_out, router_out, sem):
-    pairs = ((serve, serve_out), (fresh, fresh_out), (router, router_out), (scale, scale_out))
-    copies = [pltpu.make_async_copy(src, dst, sem.at[k]) for k, (src, dst) in enumerate(pairs)]
-    for copy in copies:
-        copy.start()
-    for copy in copies:
-        copy.wait()
+def gather_rest(serve, stored):
+    dma, any_, vmem = pltpu.SemaphoreType.DMA, pl.BlockSpec(memory_space=pl.ANY), pl.BlockSpec(memory_space=pltpu.VMEM)
+    return pl.pallas_call(
+        rest_kernel,
+        out_shape=pltpu.VMEM((REST, WIDE), BF16),
+        in_specs=[vmem, any_],
+        out_specs=vmem,
+        scratch_shapes=[dma, dma, dma((2,)), dma, dma],
+        compiler_params=pltpu.CompilerParams(
+            collective_id=1, has_side_effects=True, vmem_limit_bytes=8 << 20
+        ),
+        name="gather_rest",
+    )(pltpu.with_memory_space_constraint(serve, pltpu.VMEM), pltpu.with_memory_space_constraint(stored, pltpu.HBM))
+
+
+def store_kernel(serve, fresh, scale, router, serve_out, fresh_out, scale_out, router_out, stored, sem):
+    x, c = lax.axis_index("fsdp"), lax.rem(lax.axis_index("ep"), NC)
+    mine = pl.ds(pl.multiple_of(x * COLS, COLS), COLS)
+
+    def store_first(n):
+        left = pl.ds(n, ROWS - n)
+        copies = [
+            pltpu.make_async_copy(fresh, fresh_out, sem.at[0]),
+            pltpu.make_async_copy(scale, scale_out, sem.at[1]),
+            pltpu.make_async_copy(router, router_out, sem.at[2]),
+            pltpu.make_async_copy(serve.at[pl.ds(0, n)], serve_out.at[pl.ds(0, n)], sem.at[3]),
+            pltpu.make_async_copy(serve.at[left, mine], serve_out.at[left, mine], sem.at[4]),
+        ]
+        for copy in copies:
+            copy.start()
+        for copy in copies:
+            copy.wait()
+
+    for core, n in enumerate(RS):
+        pl.when(c == core)(lambda n=n: store_first(n))
 
 
 def store(serve, fresh, scale, router):
     vmem, any_ = pl.BlockSpec(memory_space=pltpu.VMEM), pl.BlockSpec(memory_space=pl.ANY)
     return pl.pallas_call(
         store_kernel,
-        out_shape=tuple(pltpu.HBM(v.shape, v.dtype) for v in (serve, fresh, scale, router)),
+        out_shape=(*(pltpu.HBM(v.shape, v.dtype) for v in (serve, fresh, scale, router)), pltpu.HBM((8, 128), F32)),
         in_specs=[vmem] * 4,
-        out_specs=(any_,) * 4,
-        scratch_shapes=[pltpu.SemaphoreType.DMA((4,))],
+        out_specs=(any_,) * 5,
+        scratch_shapes=[pltpu.SemaphoreType.DMA((5,))],
         compiler_params=pltpu.CompilerParams(vmem_limit_bytes=16 << 20),
         name="store",
     )(*(pltpu.with_memory_space_constraint(v, pltpu.VMEM) for v in (serve, fresh, scale, router)))
 
 
+def store_rest_kernel(rest, serve_in, serve_out, sem):
+    x, c = lax.axis_index("fsdp"), lax.rem(lax.axis_index("ep"), NC)
+
+    def store_last(first):
+        n = ROWS - first
+        copies = []
+        for k in range(1, NX):
+            lanes = pl.ds(pl.multiple_of(lax.rem(x + k, NX) * COLS, COLS), COLS)
+            src, dst = rest.at[pl.ds(0, n), lanes], serve_out.at[pl.ds(first, n), lanes]
+            copies.append(pltpu.make_async_copy(src, dst, sem.at[k - 1]))
+        for copy in copies:
+            copy.start()
+        for copy in copies:
+            copy.wait()
+
+    for core, first in enumerate(RS):
+        pl.when(c == core)(lambda first=first: store_last(first))
+
+
+def store_rest(rest, serve):
+    vmem, any_ = pl.BlockSpec(memory_space=pltpu.VMEM), pl.BlockSpec(memory_space=pl.ANY)
+    return pl.pallas_call(
+        store_rest_kernel,
+        out_shape=pltpu.HBM(serve.shape, serve.dtype),
+        in_specs=[vmem, any_],
+        out_specs=any_,
+        input_output_aliases={1: 0},
+        scratch_shapes=[pltpu.SemaphoreType.DMA((NX - 1,))],
+        compiler_params=pltpu.CompilerParams(vmem_limit_bytes=8 << 20),
+        name="store_rest",
+    )(pltpu.with_memory_space_constraint(rest, pltpu.VMEM), pltpu.with_memory_space_constraint(serve, pltpu.HBM))
+
+
 def body(w_down, avg_down, router_weight, router_gain):
-    serve, fresh, scale, router = store(
-        *gather(
-            w_down.reshape(ROWS, COLS),
-            avg_down.reshape(ROWS, COLS),
-            router_weight.reshape(1, COLS),
-            router_gain.reshape(1, COLS),
-        )
+    gathered, fresh, scale, router = gather(
+        w_down.reshape(ROWS, COLS),
+        avg_down.reshape(ROWS, COLS),
+        router_weight.reshape(1, COLS),
+        router_gain.reshape(1, COLS),
     )
+    serve, fresh, scale, router, stored = store(gathered, fresh, scale, router)
+    serve = store_rest(gather_rest(gathered, stored), serve)
     return (
         serve.reshape(1, ROWS, WIDE),
         scale,

time: 58.1 us -> 56.2 us (0.967)
  Pallas kernels: 56.9 us -> 54.4 us
    pallas_call x1, Pallas kernels: 53.4 us -> 40.6 us  [gather(): pl.pallas_call(gather_kernel, out_shape=(pltpu.VMEM((ROWS, WIDE), BF16),...]
    pallas_call x1 -> x3, Pallas kernels: 3.52 us -> 13.9 us  [the longest x1 9.6 us: gather_rest(): pl.pallas_call(rest_kernel, out_shape=pltpu.VMEM((REST, WIDE), BF16), in_...]
where the time goes in v5:
time: 56.2 us; the launch traced here: 55.1 us
  Pallas kernels  54.4 us (97%)
  between operations  0.66 us (1%)
    pallas_call x1, Pallas kernels, gather(): pl.pallas_call(gather_kernel, out_shape=(pltpu.VMEM((ROWS, WIDE), BF16),...  40.6 us
    pallas_call x1, Pallas kernels, gather_rest(): pl.pallas_call(rest_kernel, out_shape=pltpu.VMEM((REST, WIDE), BF16), in_...  9.6 us
    pallas_call x1, Pallas kernels, store(): pl.pallas_call(store_kernel, out_shape=(*(pltpu.HBM(v.shape, v.dtype) for...  3.43 us

profile of v5, /device:TPU:8, one launch (start us, length us, event | category | flops | bytes accessed | tf_op | source)
XLA Modules:
  0.0 55.1 jit_solution(4296054155318123861)
XLA Ops:
  0.6 40.6 %gather.1 = (bf16[1408,2048]{1,0:T(8,128)(2,1)S(1)}, f32[1408,512]{1,0:T(8,128)S(1)}, f32[1,1408]{1,0:T(1,128)S(1)}, bf16[8,8,2048]{2,1,0:T(8,128)(2,1)S(1)}) custom-call(f32[1408,512]{1,0:T(8,128)} %bitcast.10, f32[1408,512]{1,0:T(8,128)} %bitcast.11, f32[1,512]{1,0:T(1,128)} %bitcast.12, f32[1,512]{1,0:T(1,128)} %bitcast.13), custom_call_target="tpu_custom_call" | custom-call | tf_op jit(solution)/shard_map/gather/pallas_call | solution.py:286
  41.2 3.4 %store.1 = (bf16[1408,2048]{1,0:T(8,128)(2,1)}, f32[1408,512]{1,0:T(8,128)}, f32[1,1408]{1,0:T(1,128)}, bf16[8,8,2048]{2,1,0:T(8,128)(2,1)}, f32[8,128]{1,0:T(8,128)}) custom-call(bf16[1408,2048]{1,0:T(8,128)(2,1)S(1)} %get-tuple-element.13.serve, f32[1408,512]{1,0:T(8,128)S(1)} %get-tuple-element.14.fresh, f32[1,1408]{1,0:T(1,128)S(1)} %get-tuple-element.15.scale, ...), custom_call_target="tpu_custom_call" | custom-call | tf_op jit(solution)/shard_map/store/pallas_call | solution.py:370
  44.6 9.6 %gather_rest.1.rest = bf16[608,2048]{1,0:T(8,128)(2,1)S(1)} custom-call(bf16[1408,2048]{1,0:T(8,128)(2,1)S(1)} %get-tuple-element.13.serve, f32[8,128]{1,0:T(8,128)} %get-tuple-element.17.stored), custom_call_target="tpu_custom_call" | custom-call | tf_op jit(solution)/shard_map/gather_rest/pallas_call | solution.py:333
  54.3 0.8 %store_rest.1 = bf16[1408,2048]{1,0:T(8,128)(2,1)} custom-call(bf16[608,2048]{1,0:T(8,128)(2,1)S(1)} %gather_rest.1.rest, bf16[1408,2048]{1,0:T(8,128)(2,1)} %get-tuple-element.18.serve_in), custom_call_target="tpu_custom_call", output_to_operand_aliasing={{}: (1, {})} | custom-call | tf_op jit(solution)/shard_map/store_rest/pallas_call | solution.py:402

commit v6 on v5

--- a/solution.py
+++ b/solution.py
@@ -16,7 +16,7 @@
 NE = 48
 
 
-RS = (1232, 800)
+RS = (1072, 736)
 REST = ROWS - min(RS)
 LOADS = (0, 256, 768, 1408)
 
@@ -35,8 +35,10 @@
     mate = {"ep": e + 1 - 2 * c}
     y_up = {"ep": z * (NY * NC) + lax.rem(y + 1, NY) * NC + c}
     y_down = {"ep": z * (NY * NC) + lax.rem(y + NY - 1, NY) * NC + c}
-    z_up = {"ep": lax.rem(z + 1, NZ) * (NY * NC) + lo}
-    z_down = {"ep": lax.rem(z + NZ - 1, NZ) * (NY * NC) + lo}
+
+    def z_peer(hop):
+        return {"ep": lax.rem(z + NZ + hop, NZ) * (NY * NC) + lo}
+
 
     barrier = pltpu.get_barrier_semaphore()
     for peer in (x_peers[2], x_peers[0], x_peers[1]):
@@ -68,8 +70,8 @@
         (c == 1, c == 0, mate),
         (y < NY - 1, y == NY - 1, y_up),
         (y == 0, y > 0, y_down),
-        (z < NZ - 1, z == NZ - 1, z_up),
-        (z == 0, z > 0, z_down),
+        *((z < NZ - hop, z >= NZ - hop, z_peer(hop)) for hop in (1, 3)),
+        *((z < hop, z >= hop, z_peer(-hop)) for hop in (1, 3)),
     )
     entries, greetings = 3, 0
     for leads, follows, peer in links:
@@ -152,14 +154,9 @@
     chip = piece.at[pl.ds(y * NC, NC)]
     below = piece.at[pl.ds(lax.rem(y + NY - 1, NY) * NC, NC)]
 
-    def z_step(k):
-        for d, peer in ((0, z_up), (1, z_down)):
-            if d == 0 or k < NZ // 2 - 1:
-                plane = router.at[lax.rem(z + (NZ - k if d == 0 else k), NZ)]
-                remote(plane, plane, r3_send, r3_recv.at[k], peer).start()
-
-    def z_arrived(k):
-        wait_for(router.at[pl.ds(0, 2 if k < NZ // 2 - 1 else 1)], r3_recv.at[k])
+    def send_plane(hop, k, step):
+        plane = router.at[lax.rem(z + NZ + k, NZ)]
+        remote(plane, plane, r3_send, r3_recv.at[step], z_peer(hop)).start()
 
     wait_for(m0.at[pl.ds(0, 3)], m_recv.at[0])
     top = jnp.maximum(jnp.maximum(m0[0], m0[1]), jnp.maximum(m0[2], m0[3]))
@@ -172,12 +169,6 @@
         own(pl.ds(NE, 2 * BLK - NE), h, d).start()
     narrow(fresh, pl.ds(0, NE), mine, scales[:NE])
 
-    @pl.when(greetings > 0)
-    def _():
-        pl.semaphore_wait(greeted, greetings)
-
-    wait_for(piece.at[lo, pl.ds(0, 3)], r0_recv)
-    remote(piece.at[lo], piece.at[lo], r12_send, r1_recv, mate).start()
     wait_for(m1.at[pl.ds(0, 3)], m_recv.at[1])
 
     def narrowed(b, carry):
@@ -194,15 +185,20 @@
         for h, d in ((0, 0), (1, 1), (1, 0), (0, 1)):
             own(pl.ds(2 * BLK, n - 2 * BLK), h, d).start()
 
-    wait_for(piece.at[0], r1_recv)
-    remote(chip, chip, r12_send, r2_recv.at[0], y_up).start()
-    remote(chip, chip, r12_send, r2_recv.at[1], y_down).start()
-
     wait_for(early, e_recv)
     scales = tall(scale[:, 0:BLK])
     for d, peer in ((0, left), (1, right)):
         narrow(early.at[d], pl.ds(0, NE), peer * COLS, scales[:NE])
 
+    @pl.when(greetings > 0)
+    def _():
+        pl.semaphore_wait(greeted, greetings)
+
+    wait_for(piece.at[lo, pl.ds(0, 3)], r0_recv)
+    remote(piece.at[lo], piece.at[lo], r12_send, r1_recv, mate).start()
+    wait_for(piece.at[0], r1_recv)
+    remote(chip, chip, r12_send, r2_recv.at[0], y_up).start()
+    remote(chip, chip, r12_send, r2_recv.at[1], y_down).start()
     wait_for(chip, r2_recv.at[0])
     remote(below, below, r12_send, r2_recv.at[1], y_up).start()
     wait_for(piece.at[pl.ds(0, 2 * NC)], r2_recv.at[1])
@@ -210,10 +206,8 @@
         for k in range(WIDE // 128):
             wide[i : i + 1, k * 128 : (k + 1) * 128] = piece[i, k // 4, k % 4 : k % 4 + 1, :]
     router[z] = wide[...].astype(BF16)
-    z_step(0)
-    if NZ > 2:
-        z_arrived(0)
-        z_step(1)
+    send_plane(1, 0, 0)
+    send_plane(-1, 0, 0)
 
     @by_core
     def _(n):
@@ -221,10 +215,12 @@
             wait_for(serve.at[pl.ds(NE, n - NE), columns(0, HALF)], pass_recv.at[d])
             forward(n, d).start()
 
-    for k in range(2, NZ // 2):
-        z_arrived(k - 1)
-        z_step(k)
-    z_arrived(NZ // 2 - 1)
+    wait_for(router.at[pl.ds(0, 2)], r3_recv.at[0])
+    for k in (0, 1):
+        send_plane(3, k, 1)
+    for k in (-1, 0, 1):
+        send_plane(-3, k, 1)
+    wait_for(router.at[pl.ds(0, 5)], r3_recv.at[1])
 
     wait_for(early, e_send)
     for k, m in enumerate((m0, m1)):
@@ -318,7 +314,7 @@
             dma,
             dma((2,)),
             dma,
-            dma((NZ // 2,)),
+            dma((2,)),
             pltpu.SemaphoreType.REGULAR,
         ],
         compiler_params=pltpu.CompilerParams(

time: 56.2 us -> 54.9 us (0.977); the launches traced: 55.1 us -> 54.8 us
    pallas_call x1, Pallas kernels: 40.6 us -> 37 us  [gather(): pl.pallas_call(gather_kernel, out_shape=(pltpu.VMEM((ROWS, WIDE), BF16),...]
    pallas_call x1, Pallas kernels: 9.6 us -> 12.9 us  [gather_rest(): pl.pallas_call(rest_kernel, out_shape=pltpu.VMEM((REST, WIDE), BF16), in_...]
where the time goes in v6:
time: 54.9 us; the launch traced here: 54.8 us
  Pallas kernels  54.1 us (99%)
  between operations  0.66 us (1%)
    pallas_call x1, Pallas kernels, gather(): pl.pallas_call(gather_kernel, out_shape=(pltpu.VMEM((ROWS, WIDE), BF16),...  37 us
    pallas_call x1, Pallas kernels, gather_rest(): pl.pallas_call(rest_kernel, out_shape=pltpu.VMEM((REST, WIDE), BF16), in_...  12.9 us
    pallas_call x1, Pallas kernels, store(): pl.pallas_call(store_kernel, out_shape=(*(pltpu.HBM(v.shape, v.dtype) for...  3.27 us

profile of v6, /device:TPU:8, one launch (start us, length us, event | category | flops | bytes accessed | tf_op | source)
XLA Modules:
  0.0 54.8 jit_solution(9086918868398488169)
XLA Ops:
  0.6 37.0 %gather.1 = (bf16[1408,2048]{1,0:T(8,128)(2,1)S(1)}, f32[1408,512]{1,0:T(8,128)S(1)}, f32[1,1408]{1,0:T(1,128)S(1)}, bf16[8,8,2048]{2,1,0:T(8,128)(2,1)S(1)}) custom-call(f32[1408,512]{1,0:T(8,128)} %bitcast.10, f32[1408,512]{1,0:T(8,128)} %bitcast.11, f32[1,512]{1,0:T(1,128)} %bitcast.12, f32[1,512]{1,0:T(1,128)} %bitcast.13), custom_call_target="tpu_custom_call" | custom-call | tf_op jit(solution)/shard_map/gather/pallas_call | solution.py:282
  37.6 3.3 %store.1 = (bf16[1408,2048]{1,0:T(8,128)(2,1)}, f32[1408,512]{1,0:T(8,128)}, f32[1,1408]{1,0:T(1,128)}, bf16[8,8,2048]{2,1,0:T(8,128)(2,1)}, f32[8,128]{1,0:T(8,128)}) custom-call(bf16[1408,2048]{1,0:T(8,128)(2,1)S(1)} %get-tuple-element.13.serve, f32[1408,512]{1,0:T(8,128)S(1)} %get-tuple-element.14.fresh, f32[1,1408]{1,0:T(1,128)S(1)} %get-tuple-element.15.scale, ...), custom_call_target="tpu_custom_call" | custom-call | tf_op jit(solution)/shard_map/store/pallas_call | solution.py:366
  40.9 12.9 %gather_rest.1.rest = bf16[672,2048]{1,0:T(8,128)(2,1)S(1)} custom-call(bf16[1408,2048]{1,0:T(8,128)(2,1)S(1)} %get-tuple-element.13.serve, f32[8,128]{1,0:T(8,128)} %get-tuple-element.17.stored), custom_call_target="tpu_custom_call" | custom-call | tf_op jit(solution)/shard_map/gather_rest/pallas_call | solution.py:329
  53.8 1.0 %store_rest.1 = bf16[1408,2048]{1,0:T(8,128)(2,1)} custom-call(bf16[672,2048]{1,0:T(8,128)(2,1)S(1)} %gather_rest.1.rest, bf16[1408,2048]{1,0:T(8,128)(2,1)} %get-tuple-element.18.serve_in), custom_call_target="tpu_custom_call", output_to_operand_aliasing={{}: (1, {})} | custom-call | tf_op jit(solution)/shard_map/store_rest/pallas_call | solution.py:398

commit v7 on v6

--- a/solution.py
+++ b/solution.py
@@ -16,8 +16,9 @@
 NE = 48
 
 
-RS = (1072, 736)
-REST = ROWS - min(RS)
+PASS = (ROWS, 736)
+KEEP = (672, 736)
+REST = ROWS - min(KEEP)
 LOADS = (0, 256, 768, 1408)
 
 
@@ -148,8 +149,8 @@
         return remote(ref, ref, fwd_send, fwd_recv, x_peers[d])
 
     def by_core(do):
-        for core, n in enumerate(RS):
-            pl.when(c == core)(lambda n=n: do(n))
+        for core in range(NC):
+            pl.when(c == core)(lambda core=core: do(PASS[core], KEEP[core]))
 
     chip = piece.at[pl.ds(y * NC, NC)]
     below = piece.at[pl.ds(lax.rem(y + NY - 1, NY) * NC, NC)]
@@ -181,8 +182,8 @@
     lax.fori_loop(2, NB, narrowed, 0)
 
     @by_core
-    def _(n):
-        for h, d in ((0, 0), (1, 1), (1, 0), (0, 1)):
+    def _(passed, kept):
+        for n, h, d in ((passed, 0, 0), (passed, 1, 1), (kept, 1, 0), (kept, 0, 1)):
             own(pl.ds(2 * BLK, n - 2 * BLK), h, d).start()
 
     wait_for(early, e_recv)
@@ -210,10 +211,10 @@
     send_plane(-1, 0, 0)
 
     @by_core
-    def _(n):
+    def _(passed, kept):
         for d in range(2):
-            wait_for(serve.at[pl.ds(NE, n - NE), columns(0, HALF)], pass_recv.at[d])
-            forward(n, d).start()
+            wait_for(serve.at[pl.ds(NE, passed - NE), columns(0, HALF)], pass_recv.at[d])
+            forward(passed, d).start()
 
     wait_for(router.at[pl.ds(0, 2)], r3_recv.at[0])
     for k in (0, 1):
@@ -230,11 +231,11 @@
     wait_for(router.at[pl.ds(0, NZ - 1)], r3_send)
 
     @by_core
-    def _(n):
-        wait_for(serve.at[pl.ds(NE, n - NE), columns(0, COLS)], keep_recv)
-        wait_for(serve.at[pl.ds(NE, n - NE), columns(0, 2 * COLS)], own_send)
-        wait_for(serve.at[pl.ds(0, n), columns(0, COLS)], fwd_send)
-        wait_for(serve.at[pl.ds(0, n), columns(0, COLS)], fwd_recv)
+    def _(passed, kept):
+        wait_for(serve.at[pl.ds(NE, kept - NE), columns(0, COLS)], keep_recv)
+        wait_for(serve.at[pl.ds(0, (passed + kept) // 2 - NE), columns(0, 2 * COLS)], own_send)
+        wait_for(serve.at[pl.ds(0, passed), columns(0, COLS)], fwd_send)
+        wait_for(serve.at[pl.ds(0, passed), columns(0, COLS)], fwd_recv)
 
 
 def rest_kernel(serve, stored, rest, own_send, keep_recv, pass_recv, fwd_send, fwd_recv):
@@ -258,23 +259,26 @@
             src_ref=src, dst_ref=dst, send_sem=send, recv_sem=recv, device_id=peers[d], device_id_type=MESH
         )
 
-    def gather_rest(first):
+    def gather_rest(first, with_far):
         n = ROWS - first
         for h, d in ((0, 0), (1, 1), (1, 0), (0, 1)):
-            lanes = columns(x * COLS + h * HALF, HALF)
-            src, dst = serve.at[pl.ds(first, n), lanes], rest.at[pl.ds(0, n), lanes]
-            remote(src, dst, own_send, pass_recv.at[d] if h == d else keep_recv, d).start()
-        for d, source in ((0, left), (1, right)):
-            wait_for(n, HALF, pass_recv.at[d])
-            ref = rest.at[pl.ds(0, n), columns(source * COLS + d * HALF, HALF)]
-            remote(ref, ref, fwd_send, fwd_recv, d).start()
+            if h != d or with_far:
+                lanes = columns(x * COLS + h * HALF, HALF)
+                src, dst = serve.at[pl.ds(first, n), lanes], rest.at[pl.ds(0, n), lanes]
+                remote(src, dst, own_send, pass_recv.at[d] if h == d else keep_recv, d).start()
+        if with_far:
+            for d, source in ((0, left), (1, right)):
+                wait_for(n, HALF, pass_recv.at[d])
+                ref = rest.at[pl.ds(0, n), columns(source * COLS + d * HALF, HALF)]
+                remote(ref, ref, fwd_send, fwd_recv, d).start()
         wait_for(n, 2 * HALF, keep_recv)
-        wait_for(n, 4 * HALF, own_send)
-        wait_for(n, 2 * HALF, fwd_send)
-        wait_for(n, 2 * HALF, fwd_recv)
-
-    for core, first in enumerate(RS):
-        pl.when(c == core)(lambda first=first: gather_rest(first))
+        wait_for(n, (4 if with_far else 2) * HALF, own_send)
+        if with_far:
+            wait_for(n, 2 * HALF, fwd_send)
+            wait_for(n, 2 * HALF, fwd_recv)
+
+    for core in range(NC):
+        pl.when(c == core)(lambda core=core: gather_rest(KEEP[core], PASS[core] < ROWS))
 
 
 def gather(w_down, avg_down, rw, gain):
@@ -341,24 +345,25 @@
 
 def store_kernel(serve, fresh, scale, router, serve_out, fresh_out, scale_out, router_out, stored, sem):
     x, c = lax.axis_index("fsdp"), lax.rem(lax.axis_index("ep"), NC)
-    mine = pl.ds(pl.multiple_of(x * COLS, COLS), COLS)
-
-    def store_first(n):
-        left = pl.ds(n, ROWS - n)
-        copies = [
-            pltpu.make_async_copy(fresh, fresh_out, sem.at[0]),
-            pltpu.make_async_copy(scale, scale_out, sem.at[1]),
-            pltpu.make_async_copy(router, router_out, sem.at[2]),
-            pltpu.make_async_copy(serve.at[pl.ds(0, n)], serve_out.at[pl.ds(0, n)], sem.at[3]),
-            pltpu.make_async_copy(serve.at[left, mine], serve_out.at[left, mine], sem.at[4]),
-        ]
+
+    def columns(hop, half, width):
+        return pl.ds(pl.multiple_of(lax.rem(x + hop, NX) * COLS + half * HALF, HALF), width)
+
+    def store_first(passed, kept):
+        pairs = [(fresh, fresh_out), (scale, scale_out), (router, router_out)]
+        pieces = [(pl.ds(0, kept), pl.ds(0, WIDE)), (pl.ds(kept, ROWS - kept), columns(0, 0, COLS))]
+        if kept < passed:
+            arrived = pl.ds(kept, passed - kept)
+            pieces += [(arrived, columns(2, 0, COLS)), (arrived, columns(3, 0, HALF)), (arrived, columns(1, 1, HALF))]
+        pairs += [(serve.at[piece], serve_out.at[piece]) for piece in pieces]
+        copies = [pltpu.make_async_copy(src, dst, sem.at[k]) for k, (src, dst) in enumerate(pairs)]
         for copy in copies:
             copy.start()
         for copy in copies:
             copy.wait()
 
-    for core, n in enumerate(RS):
-        pl.when(c == core)(lambda n=n: store_first(n))
+    for core in range(NC):
+        pl.when(c == core)(lambda core=core: store_first(PASS[core], KEEP[core]))
 
 
 def store(serve, fresh, scale, router):
@@ -368,7 +373,7 @@
         out_shape=(*(pltpu.HBM(v.shape, v.dtype) for v in (serve, fresh, scale, router)), pltpu.HBM((8, 128), F32)),
         in_specs=[vmem] * 4,
         out_specs=(any_,) * 5,
-        scratch_shapes=[pltpu.SemaphoreType.DMA((5,))],
+        scratch_shapes=[pltpu.SemaphoreType.DMA((8,))],
         compiler_params=pltpu.CompilerParams(vmem_limit_bytes=16 << 20),
         name="store",
     )(*(pltpu.with_memory_space_constraint(v, pltpu.VMEM) for v in (serve, fresh, scale, router)))
@@ -377,20 +382,26 @@
 def store_rest_kernel(rest, serve_in, serve_out, sem):
     x, c = lax.axis_index("fsdp"), lax.rem(lax.axis_index("ep"), NC)
 
-    def store_last(first):
+    def columns(hop, half, width):
+        return pl.ds(pl.multiple_of(lax.rem(x + hop, NX) * COLS + half * HALF, HALF), width)
+
+    def store_last(first, with_far):
         n = ROWS - first
-        copies = []
-        for k in range(1, NX):
-            lanes = pl.ds(pl.multiple_of(lax.rem(x + k, NX) * COLS, COLS), COLS)
-            src, dst = rest.at[pl.ds(0, n), lanes], serve_out.at[pl.ds(first, n), lanes]
-            copies.append(pltpu.make_async_copy(src, dst, sem.at[k - 1]))
+        if with_far:
+            pieces = [columns(hop, 0, COLS) for hop in (1, 2, 3)]
+        else:
+            pieces = [columns(3, 1, HALF), columns(1, 0, HALF)]
+        copies = [
+            pltpu.make_async_copy(rest.at[pl.ds(0, n), lanes], serve_out.at[pl.ds(first, n), lanes], sem.at[k])
+            for k, lanes in enumerate(pieces)
+        ]
         for copy in copies:
             copy.start()
         for copy in copies:
             copy.wait()
 
-    for core, first in enumerate(RS):
-        pl.when(c == core)(lambda first=first: store_last(first))
+    for core in range(NC):
+        pl.when(c == core)(lambda core=core: store_last(KEEP[core], PASS[core] < ROWS))
 
 
 def store_rest(rest, serve):

time: 54.9 us -> 54.8 us (level)
    pallas_call x1, Pallas kernels: 12.9 us -> 9.88 us  [gather_rest(): pl.pallas_call(rest_kernel, out_shape=pltpu.VMEM((REST, WIDE), BF16), in_...]
    pallas_call x1, Pallas kernels: 37 us -> 39.9 us  [gather(): pl.pallas_call(gather_kernel, out_shape=(pltpu.VMEM((ROWS, WIDE), BF16),...]
where the time goes in v7:
time: 54.8 us; the launch traced here: 54.7 us
  Pallas kernels  54 us (99%)
  between operations  0.66 us (1%)
    pallas_call x1, Pallas kernels, gather(): pl.pallas_call(gather_kernel, out_shape=(pltpu.VMEM((ROWS, WIDE), BF16),...  39.9 us
    pallas_call x1, Pallas kernels, gather_rest(): pl.pallas_call(rest_kernel, out_shape=pltpu.VMEM((REST, WIDE), BF16), in_...  9.88 us
    pallas_call x1, Pallas kernels, store(): pl.pallas_call(store_kernel, out_shape=(*(pltpu.HBM(v.shape, v.dtype) for...  3.34 us

profile of v7, /device:TPU:8, one launch (start us, length us, event | category | flops | bytes accessed | tf_op | source)
XLA Modules:
  0.0 54.7 jit_solution(11378347114261095042)
XLA Ops:
  0.6 39.9 %gather.1 = (bf16[1408,2048]{1,0:T(8,128)(2,1)S(1)}, f32[1408,512]{1,0:T(8,128)S(1)}, f32[1,1408]{1,0:T(1,128)S(1)}, bf16[8,8,2048]{2,1,0:T(8,128)(2,1)S(1)}) custom-call(f32[1408,512]{1,0:T(8,128)} %bitcast.10, f32[1408,512]{1,0:T(8,128)} %bitcast.11, f32[1,512]{1,0:T(1,128)} %bitcast.12, f32[1,512]{1,0:T(1,128)} %bitcast.13), custom_call_target="tpu_custom_call" | custom-call | tf_op jit(solution)/shard_map/gather/pallas_call | solution.py:286
  40.5 3.3 %store.1 = (bf16[1408,2048]{1,0:T(8,128)(2,1)}, f32[1408,512]{1,0:T(8,128)}, f32[1,1408]{1,0:T(1,128)}, bf16[8,8,2048]{2,1,0:T(8,128)(2,1)}, f32[8,128]{1,0:T(8,128)}) custom-call(bf16[1408,2048]{1,0:T(8,128)(2,1)S(1)} %get-tuple-element.13.serve, f32[1408,512]{1,0:T(8,128)S(1)} %get-tuple-element.14.fresh, f32[1,1408]{1,0:T(1,128)S(1)} %get-tuple-element.15.scale, ...), custom_call_target="tpu_custom_call" | custom-call | tf_op jit(solution)/shard_map/store/pallas_call | solution.py:371
  43.9 9.9 %gather_rest.1.rest = bf16[736,2048]{1,0:T(8,128)(2,1)S(1)} custom-call(bf16[1408,2048]{1,0:T(8,128)(2,1)S(1)} %get-tuple-element.13.serve, f32[8,128]{1,0:T(8,128)} %get-tuple-element.17.stored), custom_call_target="tpu_custom_call" | custom-call | tf_op jit(solution)/shard_map/gather_rest/pallas_call | solution.py:333
  53.8 0.9 %store_rest.1 = bf16[1408,2048]{1,0:T(8,128)(2,1)} custom-call(bf16[736,2048]{1,0:T(8,128)(2,1)S(1)} %gather_rest.1.rest, bf16[1408,2048]{1,0:T(8,128)(2,1)} %get-tuple-element.18.serve_in), custom_call_target="tpu_custom_call", output_to_operand_aliasing={{}: (1, {})} | custom-call | tf_op jit(solution)/shard_map/store_rest/pallas_call | solution.py:409

commit v8 on v7

--- a/solution.py
+++ b/solution.py
@@ -16,8 +16,8 @@
 NE = 48
 
 
-PASS = (ROWS, 736)
-KEEP = (672, 736)
+PASS = (ROWS, 800)
+KEEP = (736, 800)
 REST = ROWS - min(KEEP)
 LOADS = (0, 256, 768, 1408)
 
@@ -391,9 +391,13 @@
             pieces = [columns(hop, 0, COLS) for hop in (1, 2, 3)]
         else:
             pieces = [columns(3, 1, HALF), columns(1, 0, HALF)]
+        half = n // 2
+        parts = [(lanes, start) for lanes in pieces for start in (0, half)]
         copies = [
-            pltpu.make_async_copy(rest.at[pl.ds(0, n), lanes], serve_out.at[pl.ds(first, n), lanes], sem.at[k])
-            for k, lanes in enumerate(pieces)
+            pltpu.make_async_copy(
+                rest.at[pl.ds(start, half), lanes], serve_out.at[pl.ds(first + start, half), lanes], sem.at[k]
+            )
+            for k, (lanes, start) in enumerate(parts)
         ]
         for copy in copies:
             copy.start()
@@ -412,7 +416,7 @@
         in_specs=[vmem, any_],
         out_specs=any_,
         input_output_aliases={1: 0},
-        scratch_shapes=[pltpu.SemaphoreType.DMA((NX - 1,))],
+        scratch_shapes=[pltpu.SemaphoreType.DMA((2 * (NX - 1),))],
         compiler_params=pltpu.CompilerParams(vmem_limit_bytes=8 << 20),
         name="store_rest",
     )(pltpu.with_memory_space_constraint(rest, pltpu.VMEM), pltpu.with_memory_space_constraint(serve, pltpu.HBM))

time: 54.8 us -> 54.8 us (level)
    pallas_call x1, Pallas kernels: 9.88 us -> 9.22 us  [gather_rest(): pl.pallas_call(rest_kernel, out_shape=pltpu.VMEM((REST, WIDE), BF16), in_...]
    pallas_call x1, Pallas kernels: 39.9 us -> 40.5 us  [gather(): pl.pallas_call(gather_kernel, out_shape=(pltpu.VMEM((ROWS, WIDE), BF16),...]
where the time goes in v8:
time: 54.8 us; the launch traced here: 54.7 us
  Pallas kernels  54 us (99%)
  between operations  0.66 us (1%)
    pallas_call x1, Pallas kernels, gather(): pl.pallas_call(gather_kernel, out_shape=(pltpu.VMEM((ROWS, WIDE), BF16),...  40.5 us
    pallas_call x1, Pallas kernels, gather_rest(): pl.pallas_call(rest_kernel, out_shape=pltpu.VMEM((REST, WIDE), BF16), in_...  9.22 us
    pallas_call x1, Pallas kernels, store(): pl.pallas_call(store_kernel, out_shape=(*(pltpu.HBM(v.shape, v.dtype) for...  3.36 us

profile of v8, /device:TPU:8, one launch (start us, length us, event | category | flops | bytes accessed | tf_op | source)
XLA Modules:
  0.0 54.7 jit_solution(1574434707216918037)
XLA Ops:
  0.6 40.5 %gather.1 = (bf16[1408,2048]{1,0:T(8,128)(2,1)S(1)}, f32[1408,512]{1,0:T(8,128)S(1)}, f32[1,1408]{1,0:T(1,128)S(1)}, bf16[8,8,2048]{2,1,0:T(8,128)(2,1)S(1)}) custom-call(f32[1408,512]{1,0:T(8,128)} %bitcast.10, f32[1408,512]{1,0:T(8,128)} %bitcast.11, f32[1,512]{1,0:T(1,128)} %bitcast.12, f32[1,512]{1,0:T(1,128)} %bitcast.13), custom_call_target="tpu_custom_call" | custom-call | tf_op jit(solution)/shard_map/gather/pallas_call | solution.py:286
  41.2 3.4 %store.1 = (bf16[1408,2048]{1,0:T(8,128)(2,1)}, f32[1408,512]{1,0:T(8,128)}, f32[1,1408]{1,0:T(1,128)}, bf16[8,8,2048]{2,1,0:T(8,128)(2,1)}, f32[8,128]{1,0:T(8,128)}) custom-call(bf16[1408,2048]{1,0:T(8,128)(2,1)S(1)} %get-tuple-element.13.serve, f32[1408,512]{1,0:T(8,128)S(1)} %get-tuple-element.14.fresh, f32[1,1408]{1,0:T(1,128)S(1)} %get-tuple-element.15.scale, ...), custom_call_target="tpu_custom_call" | custom-call | tf_op jit(solution)/shard_map/store/pallas_call | solution.py:371
  44.5 9.2 %gather_rest.1.rest = bf16[672,2048]{1,0:T(8,128)(2,1)S(1)} custom-call(bf16[1408,2048]{1,0:T(8,128)(2,1)S(1)} %get-tuple-element.13.serve, f32[8,128]{1,0:T(8,128)} %get-tuple-element.17.stored), custom_call_target="tpu_custom_call" | custom-call | tf_op jit(solution)/shard_map/gather_rest/pallas_call | solution.py:333
  53.8 0.9 %store_rest.1 = bf16[1408,2048]{1,0:T(8,128)(2,1)} custom-call(bf16[672,2048]{1,0:T(8,128)(2,1)S(1)} %gather_rest.1.rest, bf16[1408,2048]{1,0:T(8,128)(2,1)} %get-tuple-element.18.serve_in), custom_call_target="tpu_custom_call", output_to_operand_aliasing={{}: (1, {})} | custom-call | tf_op jit(solution)/shard_map/store_rest/pallas_call | solution.py:413
